TPU v7x, 128 devices: a whole 4x4x4 slice. The times are simulated.
128 devices in a mesh: req: 32 (over x, y, core), head: 4 (over z).
Axes of the slice: x: 4, y: 4, z: 4, core: 2. Of those that a mesh axis runs over, the one named last changes fastest.
Arguments:
- queries: bfloat16 [512, 64, 128], P('req', 'head'), may hold values from -6 to 6
- k_codes: bfloat16 [32768, 16, 8, 128], P('req', None, 'head'), may hold values from -6 to 6
- value_quantized_codes: bfloat16 [32768, 16, 8, 128], P('req', None, 'head'), may hold values from -6 to 6
- key_page_scale: float32 [32768, 8], P('req', 'head'), may hold values from 0.5 to 2
- value_page_scale: float32 [32768, 8], P('req', 'head'), may hold values from 4 to 16
- lengths: int32 [512], P('req'), may hold values from 1 to 2032
- page_table: int32 [512, 128], P('req'), may hold values from -1 to 32767, as said below
- out_weight: bfloat16 [8192, 8192], P('head', 'req'), may hold values from -0.0625 to 0.0625
Outputs:
- attn_out: bfloat16 [512, 8192], P(None, ('req', 'head'))
Inputs may be any that keep to these rules, and one draw needn't show every extreme that they name: `page_table`: entries j below ceil(lengths[r] / 16) name pool pages; all such entries of all requests together name every pool page exactly once. Entries beyond are -1.
All inputs are finite; a program needn't handle non-finite values.
Results may differ from a plain program's by a relative error of at most 0.02.
Values may be sent and summed in bfloat16 or wider, within the bound.
A program may use at most 128 MiB of HBM per device.

v0:
```python
import math

import jax
import jax.numpy as jnp
from jax import lax
from jax.sharding import PartitionSpec as P

floor_score = -1e30


def in_one_piece(arrays, axis, dim, along):
    widths = [math.prod(a.shape[along:]) for a in arrays]
    both = jnp.concatenate(
        [a.reshape(*a.shape[:along], w) for a, w in zip(arrays, widths)], axis=along
    )
    out = lax.all_gather(both, axis, axis=dim, tiled=True)
    blocks = jnp.split(out, [sum(widths[:k]) for k in range(1, len(widths))], axis=along)
    return tuple((b.reshape(*out.shape[:along], *a.shape[along:]) for a, b in zip(arrays, blocks)))


def joined_along(blocks, dim):
    lengths = list(blocks.shape[1:])
    lengths[dim] *= blocks.shape[0]
    return jnp.moveaxis(blocks, 0, dim).reshape(lengths)


def from_everyone(shard, axis):
    copies = jnp.broadcast_to(shard, (lax.axis_size(axis), *shard.shape))
    return lax.all_to_all(copies, axis, split_axis=0, concat_axis=0, tiled=True)


def collect(shard, axis, dim):
    return joined_along(from_everyone(shard, axis), dim)


def split_up(shard, dim, peers):
    before, after = (shard.shape[:dim], shard.shape[dim + 1 :])
    return jnp.moveaxis(shard.reshape(*before, peers, -1, *after), dim, 0)


def summed_on_arrival(shard, axis, dim):
    blocks = split_up(shard, dim, lax.axis_size(axis))
    arrived = lax.all_to_all(blocks, axis, split_axis=0, concat_axis=0, tiled=True)
    return arrived.astype(jnp.float32).sum(axis=0)


def split_product(member_b, data):
    high_part = data.astype(jnp.bfloat16)
    low_part = (data - high_part.astype(jnp.float32)).astype(jnp.bfloat16)
    first = jnp.dot(member_b, high_part, preferred_element_type=jnp.float32)
    return first + jnp.dot(member_b, low_part, preferred_element_type=jnp.float32)


def locate_pages(all_table, all_lengths, offset, pages_here):
    request_count, table_width = all_table.shape
    flat_ids = all_table.reshape(request_count * table_width)
    local_slot = flat_ids - offset
    inside = (flat_ids >= 0) & (local_slot >= 0) & (local_slot < pages_here)
    target = jnp.where(inside, local_slot, pages_here)
    entry_code = jnp.arange(request_count * table_width, dtype=jnp.int32)
    placed = jnp.zeros((pages_here,), jnp.int32).at[target].set(entry_code, mode="drop")
    owners = placed // table_width
    ranks = placed % table_width
    return (owners, ranks, all_lengths[owners])


def on_device(
    queries,
    k_codes,
    value_quantized_codes,
    key_page_scale,
    value_page_scale,
    lengths,
    page_table,
    out_weight,
):
    pages_here, page_size, kv_local, head_size = k_codes.shape
    rows_here = queries.shape[0]
    heads_local = queries.shape[1]
    query_group_count = heads_local // kv_local
    every_query = lax.all_gather(queries, "req", axis=0, tiled=True)
    all_lengths, all_table = in_one_piece((lengths, page_table), "req", 0, 1)
    request_count, table_width = all_table.shape
    offset = lax.axis_index("req") * pages_here
    owners, page_rank, page_length = locate_pages(all_table, all_lengths, offset, pages_here)
    position = page_rank[:, None] * page_size + jnp.arange(page_size, dtype=jnp.int32)[None, :]
    is_live = (position < page_length[:, None])[:, None, None, :]
    page_query = every_query[owners].reshape(pages_here, kv_local, query_group_count, head_size)
    scores = jnp.einsum("pkgd,ptkd->pkgt", page_query, k_codes, preferred_element_type=jnp.float32)
    scores = scores * (key_page_scale[:, :, None, None] / math.sqrt(head_size))
    page_max = jnp.max(jnp.where(is_live, scores, floor_score), axis=-1)
    weights = jnp.where(is_live, jnp.exp(scores - page_max[..., None]), 0.0).astype(jnp.bfloat16)
    page_sum = jnp.sum(weights.astype(jnp.float32), axis=-1).reshape(pages_here, heads_local)
    page_out = jnp.einsum(
        "pkgt,ptkd->pkgd", weights, value_quantized_codes, preferred_element_type=jnp.float32
    )
    page_out = (page_out * value_page_scale[:, :, None, None]).reshape(
        pages_here, heads_local, head_size
    )
    page_max = page_max.reshape(pages_here, heads_local)
    member = owners[:, None] == jnp.arange(request_count, dtype=jnp.int32)[None, :]
    local_peak = jnp.max(jnp.where(member[:, :, None], page_max[:, None, :], floor_score), axis=0)
    member_b = member.astype(jnp.bfloat16).T
    factor = jnp.exp(page_max - local_peak[owners])
    weighted = (page_out * factor[:, :, None]).reshape(pages_here, heads_local * head_size)
    numerator = split_product(member_b, weighted)
    denominator = split_product(member_b, page_sum * factor)
    numerator, denominator = (numerator, denominator)
    sources = lax.axis_size("req")
    numer_in = lax.all_to_all(
        numerator.reshape(sources, rows_here, heads_local * head_size),
        "req",
        split_axis=0,
        concat_axis=0,
        tiled=True,
    )
    denom_in = lax.all_to_all(
        denominator.reshape(sources, rows_here, heads_local),
        "req",
        split_axis=0,
        concat_axis=0,
        tiled=True,
    )
    peak_in = lax.all_to_all(
        local_peak.reshape(sources, rows_here, heads_local),
        "req",
        split_axis=0,
        concat_axis=0,
        tiled=True,
    )
    row_count = numer_in.shape[1]
    overall = jnp.max(peak_in, axis=0)
    factor = jnp.exp(peak_in - overall[None])
    numer_sum = jnp.sum(
        numer_in.reshape(sources, row_count, heads_local, head_size) * factor[..., None], axis=0
    )
    denom_sum = jnp.sum(denom_in * factor, axis=0)
    attention = (numer_sum / denom_sum[..., None]).reshape(row_count, heads_local * head_size)
    attention = attention.astype(jnp.bfloat16)
    terms = jnp.dot(collect(attention, "req", 0), out_weight, preferred_element_type=jnp.float32)
    return summed_on_arrival(terms.astype(jnp.bfloat16), "head", 1).astype(jnp.bfloat16)


def solution(mesh):
    in_specs = (
        P("req", "head", None),
        P("req", None, "head", None),
        P("req", None, "head", None),
        P("req", "head"),
        P("req", "head"),
        P("req"),
        P("req", None),
        P("head", "req"),
    )
    out_specs = P(None, ("req", "head"))
    return jax.shard_map(
        on_device, mesh=mesh, in_specs=in_specs, out_specs=out_specs, check_vma=False
    )
```

profile of v0, /device:TPU:1, one launch (start us, length us, event | category | flops | bytes accessed | tf_op | source)
XLA Modules:
  0.0 502.3 jit_solution(14878739557685162548)
XLA Ops:
  8.8 26.5 %all_gather.6 = s32[512,129]{1,0:T(8,128)S(1)} all-gather(s32[16,129]{1,0:T(8,128)S(1)} %pad_add_fusion), channel_id=1, replica_groups=mesh['req'=32,'head'=4] {'req'}, dimensions={0}, use_global_device_ids=true | all-gather | bytes 272448 | tf_op jit(solution)/shard_map/all_gather | solution.py:16
  37.3 1.8 copy.78
  39.1 239.5 %scatter_custom_fusion = s32[1024]{0:T(1024)S(1)} fusion(s32[65536]{0:T(1024)S(1)} %bitcast.99, s32[65536]{0:T(1024)S(1)} %iota.18, s32[]{:T(128)} %constant.38.clone.1), kind=kCustom, calls=%fused_computation.58 | custom fusion | bytes 4100 | tf_op jit(solution)/shard_map/scatter | solution.py:61
  278.7 6.9 %gather_fusion = s32[1024]{0:T(1024)S(1)} fusion(s32[512]{0:T(512)S(1)} %slice_reduce_fusion, s32[1024]{0:T(1024)S(1)} %get-tuple-element.7), kind=kCustom, calls=%fused_computation | custom fusion | bytes 12288 | tf_op jit(solution)/shard_map/gather | solution.py:64
  286.3 10.1 %gather_fusion.1 = bf16[1024,16,128]{2,1,0:T(8,128)(2,1)} fusion(bf16[512,16,128]{2,1,0:T(8,128)(2,1)} %all-gather.2.cloned.1.call-done, s32[1024]{0:T(1024)S(1)} %get-tuple-element.7), kind=kCustom, calls=%fused_computation.1 | custom fusion | bytes 8392704 | tf_op jit(solution)/shard_map/gather | solution.py:88
  296.4 10.4 %select_reduce_fusion.1 = (f32[1024,2,8]{2,1,0:T(2,128)S(1)}, f32[1024,2,8,16]{3,2,1,0:T(8,128)}) fusion(f32[1024,2]{1,0:T(8,128)S(1)} %copy.76, pred[1024,16]{1,0:T(8,128)(4,1)S(1)} %add_compare_fusion, bf16[1024,16,2,128]{3,2,1,0:T(2,128)(2,1)} %param.9, bf16[1024,16,128]{2,1,0:T(8,128)(2,1)} %gather_fusion.1), kind=kOutput, calls=%fused_computation.13 | convolution fusion | flops 67878912 | bytes 13721600 | tf_op jit(solution)/shard_map/pkgd,ptkd->pkgt/dot_general | solution.py:89
  308.3 5.6 %select_reduce_fusion = f32[512,16]{0,1:T(8,128)S(1)} fusion(f32[1024,16]{1,0:T(8,128)} %copy.80, pred[1024,512]{1,0:T(8,128)(4,1)S(1)} %iota_compare_fusion), kind=kLoop, calls=%fused_computation.4 | loop fusion | flops 16769024 | bytes 622592 | tf_op jit(solution)/shard_map/reduce_max | solution.py:102
  316.4 5.2 %all-to-all-start.1 = ((f32[32,1,256]{2,1,0:T(1,128)}), f32[32,1,256]{2,1,0:T(1,128)}, u32[]{:S(2)}, u32[]{:S(2)}) async-start(f32[32,1,256]{2,1,0:T(1,128)} %reshape.206), calls=%async_computation.1 | async-start | bytes 65536 | tf_op jit(solution)/shard_map/all_to_all | solution.py:124
  321.6 2.8 gather_fusion.2
  325.6 10.7 %convert_reduce_fusion = f32[1024,2,8]{2,1,0:T(2,128)} fusion(f32[1024,2,8]{2,1,0:T(2,128)S(1)} %get-tuple-element.10, f32[1024,2,8,16]{3,2,1,0:T(8,128)} %get-tuple-element.11, f32[1024,2]{1,0:T(8,128)S(1)} %copy.76, pred[1024,16]{1,0:T(8,128)(4,1)S(1)} %add_compare_fusion), kind=kLoop, calls=%fused_computation.10 | loop fusion | flops 1556480 | bytes 1204224 | tf_op jit(solution)/shard_map/reduce_sum | solution.py:93
  336.3 1.4 copy.86
  338.2 11.1 %broadcast_multiply_fusion = f32[1024,2,8,128]{3,2,1,0:T(8,128)S(1)} fusion(f32[1024,2]{1,0:T(8,128)} %copy.78, bf16[1024,16,2,128]{3,2,1,0:T(2,128)(2,1)} %param.10, f32[1024,2,8,16]{3,2,1,0:T(8,128)} %get-tuple-element.11, f32[1024,2,8]{2,1,0:T(2,128)S(1)} %get-tuple-element.10, f32[1024,2]{1,0:T(8,128)S(1)} %copy.76, ...), kind=kOutput, calls=%fused_computation.17 | convolution fusion | flops 70254592 | bytes 17924096 | tf_op jit(solution)/shard_map/pkgt,ptkd->pkgd/dot_general | solution.py:94
  349.3 2.3 mul.61
  351.6 8.5 %fusion.4 = f32[512,2048]{1,0:T(8,128)} fusion(f32[128,8,16,128]{3,2,1,0:T(8,128)S(1)} %bitcast.88, f32[128,8,16,128]{3,2,1,0:T(8,128)S(1)} %bitcast.90, s32[1024]{0:T(1024)S(1)} %get-tuple-element.8), kind=kOutput, calls=%fused_computation.14 | convolution fusion | flops 2158493696 | bytes 20975616 | tf_op jit(solution)/shard_map/dot_general | solution.py:51
  361.7 7.4 %all-to-all-start.2 = ((f32[32,1,256]{2,1,0:T(1,128)}), f32[32,1,256]{2,1,0:T(1,128)S(1)}, u32[]{:S(2)}, u32[]{:S(2)}) async-start(f32[32,1,256]{2,1,0:T(1,128)} %reshape.208), calls=%async_computation.2 | async-start | bytes 65536 | tf_op jit(solution)/shard_map/all_to_all | solution.py:117
  369.1 14.9 %convolution_add_fusion = f32[512,2048]{1,0:T(8,128)} fusion(f32[512,2048]{1,0:T(8,128)} %fusion.4, f32[128,8,16,128]{3,2,1,0:T(8,128)} %bitcast.89, f32[128,8,16,128]{3,2,1,0:T(8,128)} %bitcast.91, s32[1024]{0:T(1024)S(1)} %get-tuple-element.8), kind=kOutput, calls=%fused_computation.18 | convolution fusion | flops 2153250816 | bytes 25169920 | tf_op jit(solution)/shard_map/dot_general | solution.py:50
  384.0 7.4 %all-to-all-start = ((f32[32,16,2048]{2,1,0:T(8,128)}), f32[32,16,2048]{2,1,0:T(8,128)}, u32[]{:S(2)}, u32[]{:S(2)}) async-start(f32[32,16,2048]{2,1,0:T(8,128)} %bitcast.92), calls=%async_computation | async-start | bytes 8388608 | tf_op jit(solution)/shard_map/all_to_all | solution.py:110
  392.0 1.5 reduce.4
  394.8 2.6 mul.64
  397.4 4.9 mul.65
  402.3 41.3 %all-to-all-done = f32[32,16,2048]{2,1,0:T(8,128)} async-done(((f32[32,16,2048]{2,1,0:T(8,128)}), f32[32,16,2048]{2,1,0:T(8,128)}, u32[]{:S(2)}, u32[]{:S(2)}) %all-to-all-start) | async-done | bytes 4194336 | tf_op jit(solution)/shard_map/all_to_all | solution.py:110
  443.6 3.9 multiply_reduce_fusion
  447.9 35.0 %all_to_all.25 = bf16[32,16,2048]{2,1,0:T(8,128)(2,1)S(1)} all-to-all(bf16[32,16,2048]{2,1,0:T(8,128)(2,1)S(1)} %broadcast_in_dim.70), channel_id=1, replica_groups=mesh['req'=32,'head'=4] {'req'}, dimensions={0} | all-to-all | bytes 4194304 | tf_op jit(solution)/shard_map/all_to_all | solution.py:29
  483.6 11.2 %all_to_all.26 = bf16[4,512,64]{1,2,0:T(8,128)(2,1)S(1)} all-to-all(bf16[4,512,64]{1,2,0:T(8,128)(2,1)S(1)} %bitcast.100), channel_id=1, replica_groups=mesh['req'=32,'head'=4] {'head'}, dimensions={0} | all-to-all | bytes 524288 | tf_op jit(solution)/shard_map/all_to_all | solution.py:43
  (54 shorter events, 16.0 us)
Async XLA Ops:
  6.5 476.3 %copy-start = (bf16[2048,256]{1,0:T(8,128)(2,1)S(1)}, bf16[2048,256]{1,0:T(8,128)(2,1)}, u32[]{:S(2)}) copy-start(bf16[2048,256]{1,0:T(8,128)(2,1)} %param.15) | copy-start | bytes 3145732
  6.5 279.8 %all-gather.2.cloned.1.call-start = ((), (), s32[]{:S(2)}) async-start(), calls=%async_computation.5 | async-start | bytes 2162688 | tf_op jit(solution)/shard_map/all_gather | solution.py:81
  307.2 6.7 %copy-start.3 = (f32[1024,2,8]{0,2,1:T(8,128)}, f32[1024,2,8]{0,2,1:T(8,128)S(1)}, u32[]{:S(2)}) copy-start(f32[1024,2,8]{0,2,1:T(8,128)S(1)} %copy.79) | copy-start | bytes 196612
  313.9 0.6 copy-start.4
  316.4 45.3 %all-to-all-start.1 = ((f32[32,1,256]{2,1,0:T(1,128)}), f32[32,1,256]{2,1,0:T(1,128)}, u32[]{:S(2)}, u32[]{:S(2)}) async-start(f32[32,1,256]{2,1,0:T(1,128)} %reshape.206), calls=%async_computation.1 | async-start | bytes 65536 | tf_op jit(solution)/shard_map/all_to_all | solution.py:124
  349.3 10.8 %copy-start.2 = (f32[1024,2,8,128]{3,2,1,0:T(8,128)}, f32[1024,2,8,128]{3,2,1,0:T(8,128)S(1)}, u32[]{:S(2)}) copy-start(f32[1024,2,8,128]{3,2,1,0:T(8,128)S(1)} %broadcast_multiply_fusion) | copy-start | bytes 25165828
  351.6 8.5 %copy-start.1 = (f32[1024,16,128]{2,1,0:T(8,128)}, f32[1024,16,128]{2,1,0:T(8,128)S(1)}, u32[]{:S(2)}) copy-start(f32[1024,16,128]{2,1,0:T(8,128)S(1)} %mul.61) | copy-start | bytes 25165828
  361.7 22.3 %all-to-all-start.2 = ((f32[32,1,256]{2,1,0:T(1,128)}), f32[32,1,256]{2,1,0:T(1,128)S(1)}, u32[]{:S(2)}, u32[]{:S(2)}) async-start(f32[32,1,256]{2,1,0:T(1,128)} %reshape.208), calls=%async_computation.2 | async-start | bytes 65536 | tf_op jit(solution)/shard_map/all_to_all | solution.py:117
  384.0 59.6 %all-to-all-start = ((f32[32,16,2048]{2,1,0:T(8,128)}), f32[32,16,2048]{2,1,0:T(8,128)}, u32[]{:S(2)}, u32[]{:S(2)}) async-start(f32[32,16,2048]{2,1,0:T(8,128)} %bitcast.92), calls=%async_computation | async-start | bytes 8388608 | tf_op jit(solution)/shard_map/all_to_all | solution.py:110
Sparse Core Ops, SparseCore 0:
  9.6 47.0 all-gather.1
where the time goes:
time: 503 us; the launch traced here: 502 us
  local copies, waits for them, and re-layouts  280 us (56%)
  blocking collectives  72.6 us (14%)
  matrix products  46.6 us (9%)
  waiting for transfers between devices  42 us (8%)
  other arithmetic  27.4 us (5%)
  starting transfers between devices  20 us (4%)
  between operations  13.7 us (3%)
    scatter x1, local copies, waits for them, and re-layouts, locate_pages(): jnp.zeros((pages_here,), jnp.int32).at[target].set(entry_code, mode='drop')  239 us
    all_to_all x1, waiting for transfers between devices, on_device(): lax.all_to_all(numerator.reshape(sources, rows_here, heads_local * head_s...  41.3 us
    all_to_all x1, blocking collectives, from_everyone(): return lax.all_to_all(copies, axis, split_axis=0, concat_axis=0, tiled=True)  35 us
    all_gather x1, blocking collectives, in_one_piece(): out = lax.all_gather(both, axis, axis=dim, tiled=True)  26.5 us
    dot_general x2, matrix products, split_product(): first = jnp.dot(member_b, high_part, preferred_element_type=jnp.float32)  15.4 us
    all_to_all x1, blocking collectives, summed_on_arrival(): lax.all_to_all(blocks, axis, split_axis=0, concat_axis=0, tiled=True)  11.2 us
    dot_general x1, matrix products, on_device(): jnp.einsum('pkgt,ptkd->pkgd', weights, value_quantized_codes, preferred_e...  11.1 us
    reduce_sum x1, other arithmetic, on_device(): jnp.sum(weights.astype(jnp.float32), axis=-1)  10.7 us
  transfers between devices with their start and end apart: 4, of which 1 were waited for; matrix products, arithmetic and copies ran while one was open for 63% of the time, Pallas kernels for 0%

commit v1 on v0

--- a/solution.py
+++ b/solution.py
@@ -51,17 +51,24 @@
     return first + jnp.dot(member_b, low_part, preferred_element_type=jnp.float32)
 
 
-def locate_pages(all_table, all_lengths, offset, pages_here):
-    request_count, table_width = all_table.shape
-    flat_ids = all_table.reshape(request_count * table_width)
-    local_slot = flat_ids - offset
-    inside = (flat_ids >= 0) & (local_slot >= 0) & (local_slot < pages_here)
-    target = jnp.where(inside, local_slot, pages_here)
-    entry_code = jnp.arange(request_count * table_width, dtype=jnp.int32)
-    placed = jnp.zeros((pages_here,), jnp.int32).at[target].set(entry_code, mode="drop")
-    owners = placed // table_width
-    ranks = placed % table_width
-    return (owners, ranks, all_lengths[owners])
+def locate_pages(page_table, lengths, pages_here):
+    rows_here, table_width = page_table.shape
+    peers = lax.axis_size("req")
+    entry = jnp.arange(table_width, dtype=jnp.int32)[None, :]
+    live = jnp.clip(lengths[:, None] - 16 * entry, 0, 16)
+    row = jnp.arange(rows_here, dtype=jnp.int32)[:, None]
+    code = jnp.where(live > 0, row * 16 + live, 0).reshape(-1)
+    ids = page_table.reshape(-1)
+    highs = peers * pages_here // 128
+    in_high = (ids[None, :] >> 7) == jnp.arange(highs, dtype=jnp.int32)[:, None]
+    in_low = (ids[:, None] & 127) == jnp.arange(128, dtype=jnp.int32)[None, :]
+    coded = jnp.where(in_low, code[:, None], 0).astype(jnp.bfloat16)
+    blocks = jnp.dot(in_high.astype(jnp.bfloat16), coded, preferred_element_type=jnp.float32)
+    blocks = blocks.reshape(peers, pages_here // 128, 128)
+    found = lax.all_to_all(blocks, "req", split_axis=0, concat_axis=0, tiled=True).astype(jnp.int32)
+    source = jnp.arange(peers, dtype=jnp.int32)[:, None, None]
+    value = jnp.sum(jnp.where(found > 0, source * 256 + found - 1, 0), axis=0).reshape(pages_here)
+    return value // 16, value % 16 + 1
 
 
 def on_device(
@@ -79,13 +86,16 @@
     heads_local = queries.shape[1]
     query_group_count = heads_local // kv_local
     every_query = lax.all_gather(queries, "req", axis=0, tiled=True)
-    all_lengths, all_table = in_one_piece((lengths, page_table), "req", 0, 1)
-    request_count, table_width = all_table.shape
-    offset = lax.axis_index("req") * pages_here
-    owners, page_rank, page_length = locate_pages(all_table, all_lengths, offset, pages_here)
-    position = page_rank[:, None] * page_size + jnp.arange(page_size, dtype=jnp.int32)[None, :]
-    is_live = (position < page_length[:, None])[:, None, None, :]
-    page_query = every_query[owners].reshape(pages_here, kv_local, query_group_count, head_size)
+    request_count = every_query.shape[0]
+    owners, live_count = locate_pages(page_table, lengths, pages_here)
+    is_live = jnp.arange(page_size, dtype=jnp.int32)[None, :] < live_count[:, None]
+    is_live = is_live[:, None, None, :]
+    member = owners[:, None] == jnp.arange(request_count, dtype=jnp.int32)[None, :]
+    pick = member.astype(jnp.bfloat16)
+    page_query = jnp.dot(
+        pick, every_query.reshape(request_count, -1), preferred_element_type=jnp.float32
+    ).astype(jnp.bfloat16)
+    page_query = page_query.reshape(pages_here, kv_local, query_group_count, head_size)
     scores = jnp.einsum("pkgd,ptkd->pkgt", page_query, k_codes, preferred_element_type=jnp.float32)
     scores = scores * (key_page_scale[:, :, None, None] / math.sqrt(head_size))
     page_max = jnp.max(jnp.where(is_live, scores, floor_score), axis=-1)
@@ -98,14 +108,14 @@
         pages_here, heads_local, head_size
     )
     page_max = page_max.reshape(pages_here, heads_local)
-    member = owners[:, None] == jnp.arange(request_count, dtype=jnp.int32)[None, :]
     local_peak = jnp.max(jnp.where(member[:, :, None], page_max[:, None, :], floor_score), axis=0)
     member_b = member.astype(jnp.bfloat16).T
     factor = jnp.exp(page_max - local_peak[owners])
     weighted = (page_out * factor[:, :, None]).reshape(pages_here, heads_local * head_size)
-    numerator = split_product(member_b, weighted)
+    numerator = jnp.dot(
+        member_b, weighted.astype(jnp.bfloat16), preferred_element_type=jnp.float32
+    ).astype(jnp.bfloat16)
     denominator = split_product(member_b, page_sum * factor)
-    numerator, denominator = (numerator, denominator)
     sources = lax.axis_size("req")
     numer_in = lax.all_to_all(
         numerator.reshape(sources, rows_here, heads_local * head_size),
@@ -132,7 +142,7 @@
     overall = jnp.max(peak_in, axis=0)
     factor = jnp.exp(peak_in - overall[None])
     numer_sum = jnp.sum(
-        numer_in.reshape(sources, row_count, heads_local, head_size) * factor[..., None], axis=0
+        numer_in.astype(jnp.float32).reshape(sources, row_count, heads_local, head_size) * factor[..., None], axis=0
     )
     denom_sum = jnp.sum(denom_in * factor, axis=0)
     attention = (numer_sum / denom_sum[..., None]).reshape(row_count, heads_local * head_size)

time: 503 us -> 249 us (0.50)
  local copies, waits for them, and re-layouts: 280 us -> 26.7 us
  blocking collectives: 72.6 us -> 42.1 us
  matrix products: 46.6 us -> 59.5 us
  starting transfers between devices: 20 us -> 28.6 us
  waiting for transfers between devices: 42 us -> 50.2 us
    scatter x1 -> x0, local copies, waits for them, and re-layouts: 239 us -> none  [locate_pages(): jnp.zeros((pages_here,), jnp.int32).at[target].set(entry_code, mode='drop')]
    all_gather x1, waiting for transfers between devices: 0.02 us -> 30.1 us  [on_device(): every_query = lax.all_gather(queries, 'req', axis=0, tiled=True)]
    all_to_all x1, waiting for transfers between devices: 41.3 us -> 14.3 us  [on_device(): lax.all_to_all(numerator.reshape(sources, rows_here, heads_local * head_s...]
    all_gather x1 -> x0, blocking collectives: 26.5 us -> none  [in_one_piece(): out = lax.all_gather(both, axis, axis=dim, tiled=True)]
    dot_general x1, matrix products: 10.4 us -> 29.6 us  [on_device(): jnp.einsum('pkgd,ptkd->pkgt', page_query, k_codes, preferred_element_type...]
    gather x2 -> x0, local copies, waits for them, and re-layouts: 16.9 us -> none  [the longest x1 10.1 us: on_device(): every_query[owners]]
    dot_general x2 -> x1, matrix products: 15.4 us -> 0.5 us  [split_product(): first = jnp.dot(member_b, high_part, preferred_element_type=jnp.float32)]
    dot_general x0 -> x3, matrix products: none -> 13.3 us  [the longest x1 7.81 us: on_device(): jnp.dot(member_b, weighted.astype(jnp.bfloat16), preferred_element_type=j...]
  transfers between devices with their start and end apart: 4 -> 5, of which waited for: 1 -> 3; matrix products, arithmetic and copies ran while one was open for 63% -> 25% of each run, Pallas kernels for 0% -> 0%
where the time goes in v1:
time: 249 us; the launch traced here: 248 us
  matrix products  59.5 us (24%)
  waiting for transfers between devices  50.2 us (20%)
  blocking collectives  42.1 us (17%)
  starting transfers between devices  28.6 us (11%)
  other arithmetic  26.8 us (11%)
  local copies, waits for them, and re-layouts  26.7 us (11%)
  between operations  13.7 us (6%)
    all_to_all x1, blocking collectives, from_everyone(): return lax.all_to_all(copies, axis, split_axis=0, concat_axis=0, tiled=True)  31.8 us
    all_gather x1, waiting for transfers between devices, on_device(): every_query = lax.all_gather(queries, 'req', axis=0, tiled=True)  30.1 us
    dot_general x1, matrix products, on_device(): jnp.einsum('pkgd,ptkd->pkgt', page_query, k_codes, preferred_element_type...  29.6 us
    dot_general x1, matrix products, on_device(): jnp.einsum('pkgt,ptkd->pkgd', weights, value_quantized_codes, preferred_e...  14.8 us
    all_to_all x1, waiting for transfers between devices, on_device(): lax.all_to_all(numerator.reshape(sources, rows_here, heads_local * head_s...  14.3 us
    reduce_sum x1, other arithmetic, on_device(): jnp.sum(weights.astype(jnp.float32), axis=-1)  10.7 us
    all_to_all x1, blocking collectives, summed_on_arrival(): lax.all_to_all(blocks, axis, split_axis=0, concat_axis=0, tiled=True)  10.3 us
    all_to_all x1, starting transfers between devices, locate_pages(): lax.all_to_all(blocks, 'req', split_axis=0, concat_axis=0, tiled=True)  8.58 us
  transfers between devices with their start and end apart: 5, of which 3 were waited for; matrix products, arithmetic and copies ran while one was open for 25% of the time, Pallas kernels for 0%

profile of v1, /device:TPU:1, one launch (start us, length us, event | category | flops | bytes accessed | tf_op | source)
XLA Modules:
  0.0 247.5 jit_solution(3286600944984245735)
XLA Ops:
  8.1 1.5 fusion.17
  9.5 8.6 %all-to-all-start = ((f32[32,8,128]{2,1,0:T(8,128)}), f32[32,8,128]{2,1,0:T(8,128)S(1)}, u32[]{:S(2)}, u32[]{:S(2)}) async-start(f32[32,8,128]{2,1,0:T(8,128)} %fusion.17), calls=%async_computation | async-start | bytes 262144 | tf_op jit(solution)/shard_map/all_to_all | solution.py:68
  19.1 1.7 copy.72
  20.8 5.0 %all-to-all-done = f32[32,8,128]{2,1,0:T(8,128)S(1)} async-done(((f32[32,8,128]{2,1,0:T(8,128)}), f32[32,8,128]{2,1,0:T(8,128)S(1)}, u32[]{:S(2)}, u32[]{:S(2)}) %all-to-all-start) | async-done | bytes 131104 | tf_op jit(solution)/shard_map/all_to_all | solution.py:68
  26.5 30.1 %all-gather.2.cloned.1.call-done = bf16[512,16,128]{2,1,0:T(8,128)(2,1)} async-done(((bf16[16,16,128]{2,1,0:T(8,128)(2,1)}), bf16[512,16,128]{2,1,0:T(8,128)(2,1)}) %all-gather.2.cloned.1.call-update) | async-done | bytes 2097168 | tf_op jit(solution)/shard_map/all_gather | solution.py:88
  56.7 4.0 %convert_bitcast_fusion = bf16[128,8,16,128]{3,1,2,0:T(8,128)(2,1)S(1)} fusion(bf16[64,8,16,128]{3,2,1,0:T(8,128)(2,1)} %bitcast.114, s32[1024]{0:T(1024)S(1)} %get-tuple-element.10), kind=kOutput, calls=%fused_computation.14 | convolution fusion | flops 2150105088 | bytes 6295552 | tf_op jit(solution)/shard_map/dot_general | solution.py:95
  62.1 29.6 %select_reduce_fusion.1 = (f32[1024,2,8]{2,1,0:T(2,128)S(1)}, f32[1024,2,8,16]{3,2,1,0:T(8,128)}) fusion(f32[1024,2]{1,0:T(8,128)S(1)} %copy.70, pred[1024,16]{1,0:T(8,128)(4,1)S(1)} %iota_compare_fusion.12, bf16[1024,2,8,128]{3,2,1,0:T(8,128)(2,1)S(1)} %bitcast.103, bf16[1024,16,2,128]{3,2,1,0:T(2,128)(2,1)} %param.9), kind=kOutput, calls=%fused_computation.10 | convolution fusion | flops 67878912 | bytes 13721600 | tf_op jit(solution)/shard_map/pkgd,ptkd->pkgt/dot_general | solution.py:99
  93.2 5.6 %select_reduce_fusion = f32[512,16]{0,1:T(8,128)S(1)} fusion(f32[1024,16]{1,0:T(8,128)} %copy.74, pred[1024,512]{1,0:T(8,128)(4,1)S(1)} %iota_compare_fusion), kind=kLoop, calls=%fused_computation.1 | loop fusion | flops 16769024 | bytes 622592 | tf_op jit(solution)/shard_map/reduce_max | solution.py:111
  101.3 5.3 %all-to-all-start.2 = ((f32[32,1,256]{2,1,0:T(1,128)}), f32[32,1,256]{2,1,0:T(1,128)}, u32[]{:S(2)}, u32[]{:S(2)}) async-start(f32[32,1,256]{2,1,0:T(1,128)} %reshape.298), calls=%async_computation.2 | async-start | bytes 65536 | tf_op jit(solution)/shard_map/all_to_all | solution.py:134
  106.6 2.8 %gather_fusion = f32[1024,16]{1,0:T(8,128)S(1)} fusion(f32[512,16]{1,0:T(8,128)S(1)} %copy.75, s32[1024]{0:T(1024)S(1)} %broadcast_clamp_fusion), kind=kCustom, calls=%fused_computation | custom fusion | bytes 135168 | tf_op jit(solution)/shard_map/gather | solution.py:113
  110.6 10.7 %convert_reduce_fusion = f32[1024,2,8]{2,1,0:T(2,128)} fusion(f32[1024,2,8]{2,1,0:T(2,128)S(1)} %get-tuple-element.11, f32[1024,2,8,16]{3,2,1,0:T(8,128)} %get-tuple-element.12, f32[1024,2]{1,0:T(8,128)S(1)} %copy.70, pred[1024,16]{1,0:T(8,128)(4,1)S(1)} %iota_compare_fusion.12), kind=kLoop, calls=%fused_computation.8 | loop fusion | flops 1556480 | bytes 1204224 | tf_op jit(solution)/shard_map/reduce_sum | solution.py:103
  122.6 14.8 %broadcast_multiply_fusion = f32[1024,2,8,128]{3,2,1,0:T(8,128)} fusion(f32[1024,2]{1,0:T(8,128)S(1)} %copy-done.3, bf16[1024,16,2,128]{3,2,1,0:T(2,128)(2,1)} %param.10, f32[1024,2,8,16]{3,2,1,0:T(8,128)} %get-tuple-element.12, f32[1024,2,8]{2,1,0:T(2,128)S(1)} %get-tuple-element.11, f32[1024,2]{1,0:T(8,128)S(1)} %copy.70, ...), kind=kOutput, calls=%fused_computation.13 | convolution fusion | flops 70254592 | bytes 17924096 | tf_op jit(solution)/shard_map/pkgt,ptkd->pkgd/dot_general | solution.py:104
  139.7 7.4 %all-to-all-start.3 = ((f32[32,1,256]{2,1,0:T(1,128)}), f32[32,1,256]{2,1,0:T(1,128)S(1)}, u32[]{:S(2)}, u32[]{:S(2)}) async-start(f32[32,1,256]{2,1,0:T(1,128)} %reshape.300), calls=%async_computation.3 | async-start | bytes 65536 | tf_op jit(solution)/shard_map/all_to_all | solution.py:127
  147.1 2.3 mul.83
  150.5 7.8 %fusion.9 = bf16[512,2048]{1,0:T(8,128)(2,1)} fusion(f32[128,8,16,128]{3,2,1,0:T(8,128)S(1)} %bitcast.102, f32[128,8,16,128]{3,2,1,0:T(8,128)S(1)} %bitcast.104, s32[1024]{0:T(1024)S(1)} %get-tuple-element.10), kind=kOutput, calls=%fused_computation.15 | convolution fusion | flops 2153250816 | bytes 18878464 | tf_op jit(solution)/shard_map/dot_general | solution.py:115
  158.3 7.4 %all-to-all-start.1 = ((bf16[32,16,2048]{2,1,0:T(8,128)(2,1)}), bf16[32,16,2048]{2,1,0:T(8,128)(2,1)S(1)}, u32[]{:S(2)}, u32[]{:S(2)}) async-start(bf16[32,16,2048]{2,1,0:T(8,128)(2,1)} %bitcast.105), calls=%async_computation.1 | async-start | bytes 4194304 | tf_op jit(solution)/shard_map/all_to_all | solution.py:120
  166.2 1.5 reduce.2
  169.4 1.7 multiply_reduce_fusion.1
  172.3 2.6 %mul.86 = f32[32,16,16,128]{3,2,1,0:T(8,128)} broadcast(f32[32,16,16]{2,1,0:T(8,128)S(1)} %copy.79), dimensions={0,1,2} | broadcast | bytes 4227072 | tf_op jit(solution)/shard_map/mul | solution.py:145
  174.9 4.9 %mul.87 = f32[32,16,2048]{2,1,0:T(8,128)} reshape(f32[32,16,16,128]{3,2,1,0:T(8,128)} %mul.86) | data formatting | bytes 8388608 | tf_op jit(solution)/shard_map/mul | solution.py:145
  179.7 14.3 %all-to-all-done.1 = bf16[32,16,2048]{2,1,0:T(8,128)(2,1)S(1)} async-done(((bf16[32,16,2048]{2,1,0:T(8,128)(2,1)}), bf16[32,16,2048]{2,1,0:T(8,128)(2,1)S(1)}, u32[]{:S(2)}, u32[]{:S(2)}) %all-to-all-start.1) | async-done | bytes 2097184 | tf_op jit(solution)/shard_map/all_to_all | solution.py:120
  194.0 2.7 %multiply_reduce_fusion = f32[16,2048]{1,0:T(8,128)S(1)} fusion(f32[32,16,2048]{2,1,0:T(8,128)} %mul.87, bf16[32,16,2048]{2,1,0:T(8,128)(2,1)S(1)} %all-to-all-done.1), kind=kLoop, calls=%fused_computation.12 | loop fusion | flops 3112960 | bytes 6422528 | tf_op jit(solution)/shard_map/reduce_sum | solution.py:144
  197.2 31.8 %all_to_all.30 = bf16[32,16,2048]{2,1,0:T(8,128)(2,1)S(1)} all-to-all(bf16[32,16,2048]{2,1,0:T(8,128)(2,1)S(1)} %broadcast_in_dim.85), channel_id=1, replica_groups=mesh['req'=32,'head'=4] {'req'}, dimensions={0} | all-to-all | bytes 4194304 | tf_op jit(solution)/shard_map/all_to_all | solution.py:29
  229.7 10.3 %all_to_all.31 = bf16[4,512,64]{1,2,0:T(8,128)(2,1)S(1)} all-to-all(bf16[4,512,64]{1,2,0:T(8,128)(2,1)S(1)} %bitcast.111), channel_id=1, replica_groups=mesh['req'=32,'head'=4] {'head'}, dimensions={0} | all-to-all | bytes 524288 | tf_op jit(solution)/shard_map/all_to_all | solution.py:43
  (54 shorter events, 19.4 us)
Async XLA Ops:
  6.5 222.4 %copy-start = (bf16[2048,256]{1,0:T(8,128)(2,1)S(1)}, bf16[2048,256]{1,0:T(8,128)(2,1)}, u32[]{:S(2)}) copy-start(bf16[2048,256]{1,0:T(8,128)(2,1)} %param.15) | copy-start | bytes 3145732
  6.5 50.1 %all-gather.2.cloned.1.call-start = ((), (), s32[]{:S(2)}) async-start(), calls=%async_computation.6 | async-start | bytes 2162688 | tf_op jit(solution)/shard_map/all_gather | solution.py:88
  9.5 16.3 %all-to-all-start = ((f32[32,8,128]{2,1,0:T(8,128)}), f32[32,8,128]{2,1,0:T(8,128)S(1)}, u32[]{:S(2)}, u32[]{:S(2)}) async-start(f32[32,8,128]{2,1,0:T(8,128)} %fusion.17), calls=%async_computation | async-start | bytes 262144 | tf_op jit(solution)/shard_map/all_to_all | solution.py:68
  92.1 6.7 %copy-start.2 = (f32[1024,2,8]{0,2,1:T(8,128)}, f32[1024,2,8]{0,2,1:T(8,128)S(1)}, u32[]{:S(2)}) copy-start(f32[1024,2,8]{0,2,1:T(8,128)S(1)} %copy.73) | copy-start | bytes 196612
  98.8 0.6 copy-start.4
  101.3 38.4 %all-to-all-start.2 = ((f32[32,1,256]{2,1,0:T(1,128)}), f32[32,1,256]{2,1,0:T(1,128)}, u32[]{:S(2)}, u32[]{:S(2)}) async-start(f32[32,1,256]{2,1,0:T(1,128)} %reshape.298), calls=%async_computation.2 | async-start | bytes 65536 | tf_op jit(solution)/shard_map/all_to_all | solution.py:134
  109.6 13.0 %copy-start.3 = (f32[1024,2]{1,0:T(8,128)S(1)}, f32[1024,2]{1,0:T(8,128)}, u32[]{:S(2)}) copy-start(f32[1024,2]{1,0:T(8,128)} %copy.72) | copy-start | bytes 24580
  139.7 18.6 %all-to-all-start.3 = ((f32[32,1,256]{2,1,0:T(1,128)}), f32[32,1,256]{2,1,0:T(1,128)S(1)}, u32[]{:S(2)}, u32[]{:S(2)}) async-start(f32[32,1,256]{2,1,0:T(1,128)} %reshape.300), calls=%async_computation.3 | async-start | bytes 65536 | tf_op jit(solution)/shard_map/all_to_all | solution.py:127
  147.1 3.4 %copy-start.1 = (f32[1024,2,8,128]{3,2,1,0:T(8,128)S(1)}, f32[1024,2,8,128]{3,2,1,0:T(8,128)}, u32[]{:S(2)}) copy-start(f32[1024,2,8,128]{3,2,1,0:T(8,128)} %broadcast_multiply_fusion) | copy-start | bytes 25165828
  158.3 35.7 %all-to-all-start.1 = ((bf16[32,16,2048]{2,1,0:T(8,128)(2,1)}), bf16[32,16,2048]{2,1,0:T(8,128)(2,1)S(1)}, u32[]{:S(2)}, u32[]{:S(2)}) async-start(bf16[32,16,2048]{2,1,0:T(8,128)(2,1)} %bitcast.105), calls=%async_computation.1 | async-start | bytes 4194304 | tf_op jit(solution)/shard_map/all_to_all | solution.py:120
Sparse Core Ops, SparseCore 0:
  9.6 47.0 all-gather.1

commit v2 on v1

v2 whole, which is shorter than its diff:
```python
import functools
import math

import jax
import jax.numpy as jnp
from jax import lax
from jax.experimental import pallas as pl
from jax.experimental.pallas import tpu as pltpu
from jax.sharding import PartitionSpec as P

LOG2E = 1.4426950408889634


def local_kernel(
    steps, code_ref, ks_ref, vs_ref, q_ref, k_ref, v_ref,
    att_ref, lse_ref,
    rows_ref, live_ref, ks0_ref, ks1_ref, vs0_ref, vs1_ref,
    pick_ref, pickt_ref, qs_ref, po_ref, pm_ref, ps_ref,
):
    step = pl.program_id(0)
    f32, bf16 = jnp.float32, jnp.bfloat16
    requests = q_ref.shape[0]
    pages = k_ref.shape[0] // 32
    heads = q_ref.shape[1] // 128
    half = heads // 2
    blocks = pages // 128
    scale = LOG2E / math.sqrt(128.0)
    for b in range(blocks):
        at = step * blocks + b
        code = code_ref[pl.ds(at, 1), :]
        lanes = pl.ds(pl.multiple_of(at * 128, 128), 128)
        owner_row = jnp.floor(code * (1.0 / 16.0))
        rows_ref[0:1, :] = owner_row
        rows_ref[1:2, :] = code - 16.0 * owner_row + 1.0
        rows_ref[2:4, :] = ks_ref[:, lanes] * scale
        rows_ref[4:6, :] = vs_ref[:, lanes]
        cols = rows_ref[...].T
        here = pl.ds(b * 128, 128)
        wide = lambda i: jnp.broadcast_to(cols[:, i : i + 1], (128, 128))
        live_ref[here, :] = wide(1)
        ks0_ref[here, :] = wide(2)
        ks1_ref[here, :] = wide(3)
        vs0_ref[here, :] = wide(4)
        vs1_ref[here, :] = wide(5)
        owner = wide(0)
        where_to = pl.ds(pl.multiple_of(step * pages + b * 128, 128), 128)
        lane = lax.broadcasted_iota(jnp.int32, (128, 128), 1).astype(f32)
        for c in range(requests // 128):
            pick_ref[where_to, c * 128 : (c + 1) * 128] = jnp.where(
                owner == lane + float(c * 128), 1.0, 0.0
            ).astype(bf16)
        row = lax.broadcasted_iota(jnp.int32, (requests, 128), 0).astype(f32)
        pickt_ref[:, lanes] = jnp.where(row == owner_row, 1.0, 0.0).astype(bf16)
    mine = pl.ds(pl.multiple_of(step * pages, pages), pages)
    pick = pick_ref[mine, :]
    for n in range(heads // 2):
        got = jnp.dot(pick, q_ref[:, n * 256 : (n + 1) * 256], preferred_element_type=f32)
        for j in range(2):
            h = 2 * n + j
            qs_ref[:, h * 8 : (h + 1) * 8, :] = got[:, j * 128 : (j + 1) * 128].reshape(
                pages // 8, 8, 128
            )
    lane = lax.broadcasted_iota(jnp.int32, (8, 256), 1)
    sub = lax.broadcasted_iota(jnp.int32, (8, 256), 0)
    own = (lane >> 5) == sub
    token = ((lane & 31) >> 1).astype(f32)
    far = jnp.float32(1e9)
    token0 = jnp.where(own & ((lane & 1) == 0), token, far)
    token1 = jnp.where(own & ((lane & 1) == 1), token, far)
    lane8 = lax.broadcasted_iota(jnp.int32, (8, 128), 1)
    ones = jnp.ones((256, 128), bf16)

    def tile(g):
        p8 = pl.ds(pl.multiple_of(g * 8, 8), 8)
        kv_rows = pl.ds(pl.multiple_of(g * 256, 256), 256)
        q = qs_ref[g].astype(bf16)
        s = lax.dot_general(
            q, k_ref[kv_rows, :], (((1,), (1,)), ((), ())), preferred_element_type=f32
        )
        live = live_ref[p8, :]
        live = jnp.concatenate([live, live], axis=1)
        parts = []
        peaks = []
        for half_id, (token_id, ks) in enumerate(((token0, ks0_ref), (token1, ks1_ref))):
            keep = (token_id < live)[None]
            k8 = ks[p8, :]
            k8 = jnp.concatenate([k8, k8], axis=1)[None]
            part = s[half_id * 64 : (half_id + 1) * 64].reshape(8, 8, 256)
            part = jnp.where(keep, part * k8, -1e30)
            top = jnp.max(part, axis=2, keepdims=True)
            parts.append(jnp.exp2(part - top).reshape(64, 256).astype(bf16))
            peaks.append(top)
        weights = jnp.concatenate(parts, axis=0)
        both = jnp.concatenate([v_ref[kv_rows, :], ones], axis=1)
        out = jnp.dot(weights, both, preferred_element_type=f32)
        pm = jnp.zeros((8, 128), f32)
        ps = jnp.zeros((8, 128), f32)
        rows = pl.ds(pl.multiple_of(step * pages + g * 8, 8), 8)
        for h in range(heads):
            vs = (vs0_ref if h < half else vs1_ref)[p8, :]
            po_ref[rows, h * 128 : (h + 1) * 128] = out[h * 8 : (h + 1) * 8, 0:128] * vs
            ps = jnp.where(lane8 == h, out[h * 8 : (h + 1) * 8, 128:256], ps)
            pm = jnp.where(lane8 == h, peaks[h // half][h % half], pm)
        pm_ref[rows, :] = pm
        ps_ref[rows, :] = ps

    group = 4

    def body(i, carry):
        for u in range(group):
            tile(i * group + u)
        return carry

    lax.fori_loop(0, pages // 8 // group, body, 0)

    @pl.when(step == steps - 1)
    def _():
        pm = pm_ref[...]
        first = jnp.dot(
            pickt_ref[...], jnp.exp2(pm * (1.0 / 16.0)).astype(bf16), preferred_element_type=f32
        )
        some = first > 0.0
        coarse = jnp.where(some, 16.0 * jnp.log2(jnp.where(some, first, 1.0)), 0.0).astype(bf16)
        back = jnp.dot(pick_ref[...], coarse, preferred_element_type=f32)
        second = jnp.dot(
            pickt_ref[...], jnp.exp2((pm - back) * 0.5).astype(bf16), preferred_element_type=f32
        )
        fine = coarse.astype(f32) + 2.0 * jnp.log2(jnp.where(some, second, 1.0))
        shift = fine.astype(bf16)
        factor = jnp.exp2(pm - jnp.dot(pick_ref[...], shift, preferred_element_type=f32))
        sums = ps_ref[...] * factor
        high = sums.astype(bf16)
        low = (sums - high.astype(f32)).astype(bf16)
        den = jnp.dot(pickt_ref[...], high, preferred_element_type=f32)
        den = den + jnp.dot(pickt_ref[...], low, preferred_element_type=f32)
        safe = jnp.where(some, den, 1.0)
        lse_ref[...] = jnp.where(some, shift.astype(f32) + jnp.log2(safe), -1e30)
        ps_ref[...] = factor
        inverse = 1.0 / safe
        for n in range(heads // 2):
            cols = []
            for j in range(2):
                h = 2 * n + j
                cols.append(
                    (po_ref[:, h * 128 : (h + 1) * 128] * ps_ref[:, h : h + 1]).astype(bf16)
                )
            total = jnp.dot(
                pickt_ref[...], jnp.concatenate(cols, axis=1), preferred_element_type=f32
            )
            for j in range(2):
                h = 2 * n + j
                att_ref[:, h * 128 : (h + 1) * 128] = (
                    total[:, j * 128 : (j + 1) * 128] * inverse[:, h : h + 1]
                ).astype(bf16)


def local_attention(code, ks, vs, every_query, keys, values):
    total_pages = keys.shape[0] // 32
    steps = 4
    pages = total_pages // steps
    requests, width = every_query.shape
    vmem = pl.BlockSpec(memory_space=pltpu.VMEM)
    f32, bf16 = jnp.float32, jnp.bfloat16
    return pl.pallas_call(
        functools.partial(local_kernel, steps),
        grid=(steps,),
        out_shape=(
            jax.ShapeDtypeStruct((requests, width), bf16),
            jax.ShapeDtypeStruct((requests, 128), f32),
        ),
        in_specs=[vmem, vmem, vmem, vmem]
        + [pl.BlockSpec((pages * 32, 128), lambda t: (t, 0))] * 2,
        out_specs=(vmem, vmem),
        scratch_shapes=[pltpu.VMEM((8, 128), f32)]
        + [pltpu.VMEM((pages, 128), f32)] * 5
        + [
            pltpu.VMEM((total_pages, requests), bf16),
            pltpu.VMEM((requests, total_pages), bf16),
            pltpu.VMEM((pages // 8, 128, 128), f32),
            pltpu.VMEM((total_pages, width), f32),
            pltpu.VMEM((total_pages, 128), f32),
            pltpu.VMEM((total_pages, 128), f32),
        ],
        compiler_params=pltpu.CompilerParams(vmem_limit_bytes=60 * 1024 * 1024),
        name="local_attention",
    )(code, ks, vs, every_query, keys, values)


def joined_along(blocks, dim):
    lengths = list(blocks.shape[1:])
    lengths[dim] *= blocks.shape[0]
    return jnp.moveaxis(blocks, 0, dim).reshape(lengths)


def from_everyone(shard, axis):
    copies = jnp.broadcast_to(shard, (lax.axis_size(axis), *shard.shape))
    return lax.all_to_all(copies, axis, split_axis=0, concat_axis=0, tiled=True)


def collect(shard, axis, dim):
    return joined_along(from_everyone(shard, axis), dim)


def split_up(shard, dim, peers):
    before, after = (shard.shape[:dim], shard.shape[dim + 1 :])
    return jnp.moveaxis(shard.reshape(*before, peers, -1, *after), dim, 0)


def summed_on_arrival(shard, axis, dim):
    blocks = split_up(shard, dim, lax.axis_size(axis))
    arrived = lax.all_to_all(blocks, axis, split_axis=0, concat_axis=0, tiled=True)
    return arrived.astype(jnp.float32).sum(axis=0)


def locate_pages(page_table, lengths, pages_here):
    rows_here, table_width = page_table.shape
    peers = lax.axis_size("req")
    entry = jnp.arange(table_width, dtype=jnp.int32)[None, :]
    live = jnp.clip(lengths[:, None] - 16 * entry, 0, 16)
    row = jnp.arange(rows_here, dtype=jnp.int32)[:, None]
    code = jnp.where(live > 0, row * 16 + live, 0).reshape(-1)
    ids = page_table.reshape(-1)
    highs = peers * pages_here // 128
    in_high = (ids[None, :] >> 7) == jnp.arange(highs, dtype=jnp.int32)[:, None]
    in_low = (ids[:, None] & 127) == jnp.arange(128, dtype=jnp.int32)[None, :]
    coded = jnp.where(in_low, code[:, None], 0).astype(jnp.bfloat16)
    blocks = jnp.dot(in_high.astype(jnp.bfloat16), coded, preferred_element_type=jnp.float32)
    blocks = blocks.reshape(peers, pages_here // 128, 128)
    found = lax.all_to_all(blocks, "req", split_axis=0, concat_axis=0, tiled=True).astype(jnp.int32)
    source = jnp.arange(peers, dtype=jnp.int32)[:, None, None]
    value = jnp.sum(jnp.where(found > 0, source * 256 + found - 1, 0), axis=0)
    return value.astype(jnp.float32)


def on_device(
    queries,
    k_codes,
    value_quantized_codes,
    key_page_scale,
    value_page_scale,
    lengths,
    page_table,
    out_weight,
):
    pages_here, page_size, kv_local, head_size = k_codes.shape
    rows_here, heads_local = queries.shape[:2]
    sources = lax.axis_size("req")
    code = locate_pages(page_table, lengths, pages_here)
    every_query = lax.all_gather(queries.reshape(rows_here, -1), "req", axis=0, tiled=True)
    part, weight = local_attention(
        code,
        key_page_scale.T,
        value_page_scale.T,
        every_query,
        k_codes.reshape(-1, head_size),
        value_quantized_codes.reshape(-1, head_size),
    )
    part_in = lax.all_to_all(
        part.reshape(sources, rows_here, heads_local * head_size),
        "req",
        split_axis=0,
        concat_axis=0,
        tiled=True,
    )
    weight_in = lax.all_to_all(
        weight[:, :heads_local].reshape(sources, rows_here, heads_local),
        "req",
        split_axis=0,
        concat_axis=0,
        tiled=True,
    )
    share = jnp.exp2(weight_in - jnp.max(weight_in, axis=0)[None])
    share = share / jnp.sum(share, axis=0)[None]
    part_in = part_in.astype(jnp.float32).reshape(sources, rows_here, heads_local, head_size)
    attention = jnp.sum(part_in * share[..., None], axis=0).reshape(rows_here, -1)
    attention = attention.astype(jnp.bfloat16)
    terms = jnp.dot(collect(attention, "req", 0), out_weight, preferred_element_type=jnp.float32)
    return summed_on_arrival(terms.astype(jnp.bfloat16), "head", 1).astype(jnp.bfloat16)


def solution(mesh):
    in_specs = (
        P("req", "head", None),
        P("req", None, "head", None),
        P("req", None, "head", None),
        P("req", "head"),
        P("req", "head"),
        P("req"),
        P("req", None),
        P("head", "req"),
    )
    out_specs = P(None, ("req", "head"))
    return jax.shard_map(
        on_device, mesh=mesh, in_specs=in_specs, out_specs=out_specs, check_vma=False
    )
```

time: 249 us -> 188 us (0.76)
  matrix products: 59.5 us -> 2.23 us
  Pallas kernels: 0 us -> 31.1 us
  other arithmetic: 26.8 us -> 5.72 us
  starting transfers between devices: 28.6 us -> 12.6 us
  local copies, waits for them, and re-layouts: 26.7 us -> 11 us
  blocking collectives: 42.1 us -> 54.4 us
  waiting for transfers between devices: 50.2 us -> 56.4 us
    dot_general x6 -> x0, matrix products: 57.3 us -> none  [the longest x1 29.6 us: on_device(): jnp.einsum('pkgd,ptkd->pkgt', page_query, k_codes, preferred_element_type...]
    pallas_call x0 -> x1, Pallas kernels: none -> 31.1 us  [local_attention(): pl.pallas_call(functools.partial(local_kernel, steps), grid=(steps,), out...]
    all_to_all x3 -> x1, starting transfers between devices: 20.1 us -> 4.06 us  [on_device(): lax.all_to_all(part.reshape(sources, rows_here, heads_local * head_size),...]
    reduce_sum x4 -> x3, other arithmetic: 15.2 us -> 2.85 us  [the longest x1 2.68 us: on_device(): jnp.sum(part_in * share[..., None], axis=0).reshape(rows_here, -1)]
    all_to_all x0 -> x1, blocking collectives: none -> 12.3 us  [on_device(): lax.all_to_all(weight[:, :heads_local].reshape(sources, rows_here, heads_...]
    reduce_max x2 -> x1, other arithmetic: 5.62 us -> 0.04 us  [on_device(): share = jnp.exp2(weight_in - jnp.max(weight_in, axis=0)[None])]
    all_to_all x3 -> x1, waiting for transfers between devices: 14.3 us -> 19.4 us  [on_device(): lax.all_to_all(part.reshape(sources, rows_here, heads_local * head_size),...]
    unnamed x16 -> x5, local copies, waits for them, and re-layouts: 7.23 us -> 2.79 us
  transfers between devices with their start and end apart: 5 -> 3, of which waited for: 3 -> 3; matrix products, arithmetic and copies ran while one was open for 25% -> 6% of each run, Pallas kernels for 0% -> 0%
where the time goes in v2:
time: 188 us; the launch traced here: 187 us
  waiting for transfers between devices  56.4 us (30%)
  blocking collectives  54.4 us (29%)
  Pallas kernels  31.1 us (17%)
  between operations  13.5 us (7%)
  starting transfers between devices  12.6 us (7%)
  local copies, waits for them, and re-layouts  11 us (6%)
  other arithmetic  5.72 us (3%)
  matrix products  2.23 us (1%)
    all_to_all x1, blocking collectives, from_everyone(): return lax.all_to_all(copies, axis, split_axis=0, concat_axis=0, tiled=True)  31.8 us
    pallas_call x1, Pallas kernels, local_attention(): pl.pallas_call(functools.partial(local_kernel, steps), grid=(steps,), out...  31.1 us
    all_gather x1, waiting for transfers between devices, on_device(): lax.all_gather(queries.reshape(rows_here, -1), 'req', axis=0, tiled=True)  29.3 us
    all_to_all x1, waiting for transfers between devices, on_device(): lax.all_to_all(part.reshape(sources, rows_here, heads_local * head_size),...  19.4 us
    all_to_all x1, blocking collectives, on_device(): lax.all_to_all(weight[:, :heads_local].reshape(sources, rows_here, heads_...  12.3 us
    all_to_all x1, blocking collectives, summed_on_arrival(): lax.all_to_all(blocks, axis, split_axis=0, concat_axis=0, tiled=True)  10.3 us
    all_to_all x1, starting transfers between devices, locate_pages(): lax.all_to_all(blocks, 'req', split_axis=0, concat_axis=0, tiled=True)  8.58 us
    all_to_all x1, waiting for transfers between devices, locate_pages(): lax.all_to_all(blocks, 'req', split_axis=0, concat_axis=0, tiled=True)  7.67 us
  transfers between devices with their start and end apart: 3, of which 3 were waited for; matrix products, arithmetic and copies ran while one was open for 6% of the time, Pallas kernels for 0%

profile of v2, /device:TPU:1, one launch (start us, length us, event | category | flops | bytes accessed | tf_op | source)
XLA Modules:
  0.0 186.9 jit_solution(2876245357396922247)
XLA Ops:
  6.5 1.6 copy.11
  8.2 0.8 and_bitcast_fusion
  8.9 1.5 fusion.1
  10.4 8.6 %all-to-all-start = ((f32[32,8,128]{2,1,0:T(8,128)}), f32[32,8,128]{2,1,0:T(8,128)S(1)}, u32[]{:S(2)}, u32[]{:S(2)}) async-start(f32[32,8,128]{2,1,0:T(8,128)} %fusion.1), calls=%async_computation | async-start | bytes 262144 | tf_op jit(solution)/shard_map/all_to_all | solution.py:229
  19.0 7.7 %all-to-all-done = f32[32,8,128]{2,1,0:T(8,128)S(1)} async-done(((f32[32,8,128]{2,1,0:T(8,128)}), f32[32,8,128]{2,1,0:T(8,128)S(1)}, u32[]{:S(2)}, u32[]{:S(2)}) %all-to-all-start) | async-done | bytes 131104 | tf_op jit(solution)/shard_map/all_to_all | solution.py:229
  26.7 0.1 select_reduce_fusion
  26.8 0.6 convert_element_type.23.code_ref
  27.4 29.3 %all-gather.2.cloned.1.call-done.q_ref = bf16[512,2048]{1,0:T(8,128)(2,1)} async-done(((bf16[16,2048]{1,0:T(8,128)(2,1)}), bf16[512,2048]{1,0:T(8,128)(2,1)}) %all-gather.2.cloned.1.call-update) | async-done | bytes 2097168 | tf_op jit(solution)/shard_map/all_gather | solution.py:249
  56.7 31.1 %local_attention.1 = (bf16[512,2048]{1,0:T(8,128)(2,1)}, f32[512,128]{1,0:T(8,128)}) custom-call(f32[8,128]{1,0:T(8,128)} %convert_element_type.23.code_ref, f32[2,1024]{1,0:T(2,128)} %bitcast.35, f32[2,1024]{1,0:T(2,128)} %bitcast.36, bf16[512,2048]{1,0:T(8,128)(2,1)} %all-gather.2.cloned.1.call-done.q_ref, bf16[32768,128]{1,0:T(8,128)(2,1)} %bitcast.27, ...), custom_call_target="tpu_custom_call" | custom-call | tf_op jit(solution)/shard_map/local_attention/pallas_call | solution.py:164
  87.7 1.1 reshape.106
  88.8 12.3 %all_to_all.25 = f32[32,1,256]{2,1,0:T(1,128)S(1)} all-to-all(f32[32,1,256]{2,1,0:T(1,128)S(1)} %reshape.106), channel_id=1, replica_groups=mesh['req'=32,'head'=4] {'req'}, dimensions={0} | all-to-all | bytes 65536 | tf_op jit(solution)/shard_map/all_to_all | solution.py:265
  101.1 4.1 %all-to-all-start.1 = ((bf16[32,16,2048]{2,1,0:T(8,128)(2,1)}), bf16[32,16,2048]{2,1,0:T(8,128)(2,1)S(1)}, u32[]{:S(2)}, u32[]{:S(2)}) async-start(bf16[32,16,2048]{2,1,0:T(8,128)(2,1)} %bitcast.29), calls=%async_computation.1 | async-start | bytes 4194304 | tf_op jit(solution)/shard_map/all_to_all | solution.py:258
  105.2 0.5 broadcast.75
  105.7 0.7 reduce.2
  106.4 0.1 reshape.107
  106.7 2.6 %mul.46 = f32[32,16,16,128]{3,2,1,0:T(8,128)} broadcast(f32[32,16,16]{2,1,0:T(8,128)S(1)} %fusion.6), dimensions={0,1,2} | broadcast | bytes 4227072 | tf_op jit(solution)/shard_map/mul | solution.py:275
  109.3 4.9 %mul.47 = f32[32,16,2048]{2,1,0:T(8,128)} reshape(f32[32,16,16,128]{3,2,1,0:T(8,128)} %mul.46) | data formatting | bytes 8388608 | tf_op jit(solution)/shard_map/mul | solution.py:275
  114.2 19.4 %all-to-all-done.1 = bf16[32,16,2048]{2,1,0:T(8,128)(2,1)S(1)} async-done(((bf16[32,16,2048]{2,1,0:T(8,128)(2,1)}), bf16[32,16,2048]{2,1,0:T(8,128)(2,1)S(1)}, u32[]{:S(2)}, u32[]{:S(2)}) %all-to-all-start.1) | async-done | bytes 2097184 | tf_op jit(solution)/shard_map/all_to_all | solution.py:258
  133.6 2.7 %multiply_reduce_fusion = bf16[16,2048]{1,0:T(8,128)(2,1)S(1)} fusion(f32[32,16,2048]{2,1,0:T(8,128)} %mul.47, bf16[32,16,2048]{2,1,0:T(8,128)(2,1)S(1)} %all-to-all-done.1), kind=kLoop, calls=%fused_computation | loop fusion | flops 3112960 | bytes 6356992 | tf_op jit(solution)/shard_map/reduce_sum | solution.py:275
  136.3 0.2 broadcast_in_dim.20
  136.6 31.8 %all_to_all.26 = bf16[32,16,2048]{2,1,0:T(8,128)(2,1)S(1)} all-to-all(bf16[32,16,2048]{2,1,0:T(8,128)(2,1)S(1)} %broadcast_in_dim.20), channel_id=1, replica_groups=mesh['req'=32,'head'=4] {'req'}, dimensions={0} | all-to-all | bytes 4194304 | tf_op jit(solution)/shard_map/all_to_all | solution.py:197
  168.3 0.8 convolution_convert_fusion
  169.1 10.3 %all_to_all.27 = bf16[4,512,64]{1,2,0:T(8,128)(2,1)S(1)} all-to-all(bf16[4,512,64]{1,2,0:T(8,128)(2,1)S(1)} %bitcast.32), channel_id=1, replica_groups=mesh['req'=32,'head'=4] {'head'}, dimensions={0} | all-to-all | bytes 524288 | tf_op jit(solution)/shard_map/all_to_all | solution.py:211
  179.4 0.7 reduce_sum.42
  (10 shorter events, 0.2 us)
Async XLA Ops:
  6.5 161.8 %copy-start = (bf16[2048,256]{1,0:T(8,128)(2,1)S(1)}, bf16[2048,256]{1,0:T(8,128)(2,1)}, u32[]{:S(2)}) copy-start(bf16[2048,256]{1,0:T(8,128)(2,1)} %param.15) | copy-start | bytes 3145732
  6.5 50.1 %all-gather.2.cloned.1.call-start = ((), (), s32[]{:S(2)}) async-start(), calls=%async_computation.5 | async-start | bytes 2162688 | tf_op jit(solution)/shard_map/all_gather | solution.py:249
  10.4 16.3 %all-to-all-start = ((f32[32,8,128]{2,1,0:T(8,128)}), f32[32,8,128]{2,1,0:T(8,128)S(1)}, u32[]{:S(2)}, u32[]{:S(2)}) async-start(f32[32,8,128]{2,1,0:T(8,128)} %fusion.1), calls=%async_computation | async-start | bytes 262144 | tf_op jit(solution)/shard_map/all_to_all | solution.py:229
  101.1 32.5 %all-to-all-start.1 = ((bf16[32,16,2048]{2,1,0:T(8,128)(2,1)}), bf16[32,16,2048]{2,1,0:T(8,128)(2,1)S(1)}, u32[]{:S(2)}, u32[]{:S(2)}) async-start(bf16[32,16,2048]{2,1,0:T(8,128)(2,1)} %bitcast.29), calls=%async_computation.1 | async-start | bytes 4194304 | tf_op jit(solution)/shard_map/all_to_all | solution.py:258
Sparse Core Ops, SparseCore 0:
  9.6 47.0 all-gather.1

commit v3 on v2

--- a/solution.py
+++ b/solution.py
@@ -11,9 +11,384 @@
 LOG2E = 1.4426950408889634
 
 
+MESH = pl.DeviceIdType.MESH
+
+
+def place():
+    me = lax.axis_index("req")
+    return lax.div(me, 8), lax.rem(lax.div(me, 2), 4), lax.rem(me, 2)
+
+
+def off(i, d):
+    return lax.rem(i + d + 4, 4)
+
+
+def chip(x, y, c):
+    return {"req": (x * 4 + y) * 2 + c}
+
+
+class Copies:
+    def __init__(self, send_sems, recv_sems):
+        self.sems, self.count, self.sent = (send_sems, recv_sems), 0, []
+
+    def send(self, source, target, device, landing):
+        pair = (self.sems[0].at[self.count], self.sems[1].at[self.count])
+        self.count += 1
+        copy = pltpu.make_async_remote_copy(source, target, *pair, device, device_id_type=MESH)
+        copy.start()
+        self.sent.append(copy)
+        return pltpu.make_async_remote_copy(source, landing, *pair, device, device_id_type=MESH)
+
+    def drain(self):
+        for copy in self.sent:
+            copy.wait_send()
+
+
+def greet(x, y, c, others=()):
+    barrier = pltpu.get_barrier_semaphore()
+    peers = [chip(off(x, d), y, c) for d in (1, 2, 3)]
+    peers += [chip(x, off(y, d), c) for d in (1, 2, 3)]
+    peers += [chip(x, y, 1 - c)] + list(others)
+    for peer in peers:
+        pl.semaphore_signal(barrier, inc=1, device_id=peer, device_id_type=MESH)
+    pl.semaphore_wait(barrier, len(peers))
+
+
+def gather_first(copies, own, view, x, y, c, halves):
+    left, right = halves
+    waits = []
+    for d in (2, 1, 3):
+        waits.append(
+            copies.send(
+                own.at[:, left], view(x, y, c, left), chip(x, off(y, d), c),
+                view(x, off(y, -d), c, left),
+            )
+        )
+        waits.append(
+            copies.send(
+                own.at[:, right], view(x, y, c, right), chip(off(x, d), y, c),
+                view(off(x, -d), y, c, right),
+            )
+        )
+    return waits
+
+
+def gather_second(copies, view, x, y, c, halves):
+    left, right = halves
+    every = slice(None)
+    waits = []
+    for d in (2, 1, 3):
+        waits.append(
+            copies.send(
+                view(x, every, c, left), view(x, every, c, left), chip(off(x, d), y, c),
+                view(off(x, -d), every, c, left),
+            )
+        )
+        waits.append(
+            copies.send(
+                view(every, y, c, right), view(every, y, c, right), chip(x, off(y, d), c),
+                view(every, off(y, -d), c, right),
+            )
+        )
+    return waits
+
+
+def gather_third(copies, waits, view, x, y, c, halves):
+    left, right = halves
+    every = slice(None)
+    twin = chip(x, y, 1 - c)
+    last = []
+
+    def pass_on(piece, theirs):
+        last.append(copies.send(piece, piece, twin, theirs))
+
+    pass_on(view(x, every, c, left), view(x, every, 1 - c, left))
+    pass_on(view(every, y, c, right), view(every, y, 1 - c, right))
+    for k, d in enumerate((2, 1, 3)):
+        waits[2 * k].wait_recv()
+        row = off(x, -d)
+        pass_on(view(row, every, c, left), view(row, every, 1 - c, left))
+        waits[2 * k + 1].wait_recv()
+        row = off(y, -d)
+        pass_on(view(every, row, c, right), view(every, row, 1 - c, right))
+    return last
+
+
+def gather_kernel(
+    lengths_ref, q_ref, table_ref, all_ref, code_ref,
+    table_out, sum_y, sum_c, in_x, in_y, in_c, send_sems, recv_sems,
+):
+    f32, bf16 = jnp.float32, jnp.bfloat16
+    x, y, c = place()
+    rows, width = q_ref.shape
+    halves = (slice(0, width // 2), slice(width // 2, width))
+
+    def view(i, j, k, cols):
+        return all_ref.at[k, i, j, :, cols]
+
+    greet(x, y, c)
+    copies = Copies(send_sems, recv_sems)
+    first = gather_first(copies, q_ref, view, x, y, c, halves)
+    all_ref[c, x, y] = q_ref[...]
+    lane = lax.broadcasted_iota(jnp.int32, (1, 128), 1)
+    high_id = lax.broadcasted_iota(jnp.int32, (256, 128), 0)
+    low_id = lax.broadcasted_iota(jnp.int32, (128, 128), 0)
+    highs, lows = [], []
+    for r in range(rows):
+        live = jnp.clip(lengths_ref[r] - 16 * lane, 0, 16)
+        coded = jnp.where(live > 0, live + 16 * r, 0).astype(f32)
+        ids = table_ref[r : r + 1, :]
+        highs.append(jnp.where(high_id == (ids >> 7), 1.0, 0.0).astype(bf16))
+        lows.append(jnp.where(low_id == (ids & 127), coded, 0.0).astype(bf16))
+    found = lax.dot_general(
+        jnp.concatenate(highs, axis=1), jnp.concatenate(lows, axis=1),
+        (((1,), (1,)), ((), ())), preferred_element_type=f32,
+    )
+    base = ((c * 16 + x * 4 + y) * 256).astype(f32)
+    table_out[...] = jnp.where(found > 0.0, found + base, 0.0).reshape(4, 4, 2, 8, 128)
+    got = [
+        copies.send(
+            table_out.at[off(x, d)], in_x.at[d - 1], chip(off(x, d), y, c), in_x.at[d - 1]
+        )
+        for d in (2, 1, 3)
+    ]
+    for wait in first:
+        wait.wait_recv()
+    second = gather_second(copies, view, x, y, c, halves)
+    for wait in got:
+        wait.wait_recv()
+    sum_y[...] = table_out[x] + in_x[0] + in_x[1] + in_x[2]
+    got = [
+        copies.send(sum_y.at[off(y, d)], in_y.at[d - 1], chip(x, off(y, d), c), in_y.at[d - 1])
+        for d in (2, 1, 3)
+    ]
+    for wait in got:
+        wait.wait_recv()
+    sum_c[...] = sum_y[y] + in_y[0] + in_y[1] + in_y[2]
+    got = copies.send(sum_c.at[1 - c], in_c, chip(x, y, 1 - c), in_c)
+    third = gather_third(copies, second, view, x, y, c, halves)
+    got.wait_recv()
+    code_ref[...] = sum_c[c] + in_c[...] - 1.0
+    for wait in third:
+        wait.wait_recv()
+    copies.drain()
+
+
+def gather_inputs(lengths, queries, page_table):
+    rows, width = queries.shape
+    f32 = jnp.float32
+    vmem = pl.BlockSpec(memory_space=pltpu.VMEM)
+    return pl.pallas_call(
+        gather_kernel,
+        out_shape=(
+            jax.ShapeDtypeStruct((2, 4, 4, rows, width), queries.dtype),
+            jax.ShapeDtypeStruct((8, 128), f32),
+        ),
+        in_specs=[pl.BlockSpec(memory_space=pltpu.SMEM), vmem, vmem],
+        out_specs=(vmem, vmem),
+        scratch_shapes=[
+            pltpu.VMEM((4, 4, 2, 8, 128), f32),
+            pltpu.VMEM((4, 2, 8, 128), f32),
+            pltpu.VMEM((2, 8, 128), f32),
+            pltpu.VMEM((3, 4, 2, 8, 128), f32),
+            pltpu.VMEM((3, 2, 8, 128), f32),
+            pltpu.VMEM((8, 128), f32),
+            pltpu.SemaphoreType.DMA((27,)),
+            pltpu.SemaphoreType.DMA((27,)),
+        ],
+        compiler_params=pltpu.CompilerParams(
+            collective_id=1, has_side_effects=True, vmem_limit_bytes=32 * 1024 * 1024
+        ),
+        name="gather_inputs",
+    )(lengths, queries, page_table)
+
+
+def unpack_log(aux):
+    aux = aux.astype(jnp.float32)
+    return aux + pltpu.roll(aux, 112, 1) + pltpu.roll(aux, 96, 1)
+
+
+def pack_log(value):
+    f32, bf16 = jnp.float32, jnp.bfloat16
+    high = value.astype(bf16).astype(f32)
+    middle = (value - high).astype(bf16).astype(f32)
+    low = value - high - middle
+    lane = lax.broadcasted_iota(jnp.int32, value.shape, 1)
+    low = jnp.where(lane < 48, pltpu.roll(low, 32, 1), 0.0)
+    low = jnp.where(lane < 32, pltpu.roll(middle, 16, 1), low)
+    return jnp.where(lane < 16, high, low).astype(bf16)
+
+
+def merged(blocks, first_head):
+    logs = [unpack_log(b[:, 1024:1152]) for b in blocks]
+    top = functools.reduce(jnp.maximum, logs)
+    shares = [jnp.exp2(g - top) for g in logs]
+    total = functools.reduce(jnp.add, shares)
+    inverse = 1.0 / total
+    shares = [s * inverse for s in shares]
+    columns = []
+    for h in range(8):
+        at = first_head + h
+        columns.append(
+            functools.reduce(
+                jnp.add,
+                [
+                    b[:, h * 128 : (h + 1) * 128].astype(jnp.float32) * s[:, at : at + 1]
+                    for b, s in zip(blocks, shares)
+                ],
+            ).astype(jnp.bfloat16)
+        )
+    return columns, top + jnp.log2(total)
+
+
+def store_merged(target, index, start, blocks, first_head):
+    columns, log = merged(blocks, first_head)
+    for h, column in enumerate(columns):
+        target[index + (slice(None), slice(start + h * 128, start + (h + 1) * 128))] = column
+    if target.shape[-1] != 2048:
+        target[index + (slice(None), slice(start + 1024, start + 1152))] = pack_log(log)
+
+
+def combine_kernel(
+    part_ref, weight_ref, out_ref,
+    twin_in, now, in_left, in_right, left_now, right_now, in_left2, in_right2,
+    own, all_ref, terms, turned, send_sems, recv_sems,
+):
+    f32, bf16 = jnp.float32, jnp.bfloat16
+    x, y, c = place()
+    z = lax.axis_index("head")
+    every = slice(None)
+    wide = 1152
+    left, right = slice(0, wide), slice(wide, 2 * wide)
+    greet(x, y, c, [{"head": off(z, d)} for d in (1, 2, 3)])
+    copies = Copies(send_sems, recv_sems)
+    twin = [
+        copies.send(part_ref.at[1 - c, i], twin_in.at[i], chip(x, y, 1 - c), twin_in.at[i])
+        for i in range(4)
+    ]
+    for k in range(16):
+        turned[:, k * 128 : (k + 1) * 128] = weight_ref[k * 128 : (k + 1) * 128, :].T
+    for i in range(4):
+        twin[i].wait_recv()
+
+        def body(j, carry):
+            for start, head in ((0, 0), (wide, 8)):
+                cols = slice(start, start + wide)
+                store_merged(
+                    now, (i, j), start, [part_ref[c, i, j, :, cols], twin_in[i, j, :, cols]], head
+                )
+            return carry
+
+        lax.fori_loop(0, 4, body, 0)
+    waits = []
+    for d in (2, 1, 3):
+        waits.append(
+            copies.send(
+                now.at[off(x, d), :, :, left], in_left.at[d - 1], chip(off(x, d), y, c),
+                in_left.at[d - 1],
+            )
+        )
+        waits.append(
+            copies.send(
+                now.at[:, off(y, d), :, right], in_right.at[d - 1], chip(x, off(y, d), c),
+                in_right.at[d - 1],
+            )
+        )
+    for wait in waits:
+        wait.wait_recv()
+
+    def body(j, carry):
+        store_merged(
+            left_now, (j,), 0, [now[x, j, :, left]] + [in_left[d, j] for d in range(3)], 0
+        )
+        store_merged(
+            right_now, (j,), 0, [now[j, y, :, right]] + [in_right[d, j] for d in range(3)], 8
+        )
+        return carry
+
+    lax.fori_loop(0, 4, body, 0)
+    waits = []
+    for d in (2, 1, 3):
+        waits.append(
+            copies.send(
+                left_now.at[off(y, d)], in_left2.at[d - 1], chip(x, off(y, d), c),
+                in_left2.at[d - 1],
+            )
+        )
+        waits.append(
+            copies.send(
+                right_now.at[off(x, d)], in_right2.at[d - 1], chip(off(x, d), y, c),
+                in_right2.at[d - 1],
+            )
+        )
+    for wait in waits:
+        wait.wait_recv()
+    store_merged(own, (), 0, [left_now[y]] + [in_left2[d] for d in range(3)], 0)
+    store_merged(own, (), 1024, [right_now[x]] + [in_right2[d] for d in range(3)], 8)
+
+    def view(i, j, k, cols):
+        return all_ref.at[i, j, k, :, cols]
+
+    halves = (slice(0, 1024), slice(1024, 2048))
+    first = gather_first(copies, own, view, x, y, c, halves)
+    all_ref[x, y, c] = own[...]
+    for wait in first:
+        wait.wait_recv()
+    second = gather_second(copies, view, x, y, c, halves)
+    for wait in gather_third(copies, second, view, x, y, c, halves):
+        wait.wait_recv()
+    attention = all_ref[...].reshape(512, 2048)
+    terms[...] = (
+        lax.dot_general(
+            turned[...], attention, (((1,), (1,)), ((), ())), preferred_element_type=f32
+        )
+        .astype(bf16)
+        .reshape(4, 64, 512)
+    )
+    waits = [
+        copies.send(terms.at[off(z, d)], out_ref.at[d], {"head": off(z, d)}, out_ref.at[d])
+        for d in (2, 1, 3)
+    ]
+    out_ref[0] = terms[z]
+    for wait in waits:
+        wait.wait_recv()
+    copies.drain()
+
+
+def combine(part, weight):
+    bf16 = jnp.bfloat16
+    vmem = pl.BlockSpec(memory_space=pltpu.VMEM)
+    return pl.pallas_call(
+        combine_kernel,
+        out_shape=jax.ShapeDtypeStruct((4, 64, 512), bf16),
+        in_specs=[vmem, vmem],
+        out_specs=vmem,
+        scratch_shapes=[
+            pltpu.VMEM((4, 4, 16, 2304), bf16),
+            pltpu.VMEM((4, 4, 16, 2304), bf16),
+            pltpu.VMEM((3, 4, 16, 1152), bf16),
+            pltpu.VMEM((3, 4, 16, 1152), bf16),
+            pltpu.VMEM((4, 16, 1152), bf16),
+            pltpu.VMEM((4, 16, 1152), bf16),
+            pltpu.VMEM((3, 16, 1152), bf16),
+            pltpu.VMEM((3, 16, 1152), bf16),
+            pltpu.VMEM((16, 2048), bf16),
+            pltpu.VMEM((4, 4, 2, 16, 2048), bf16),
+            pltpu.VMEM((4, 64, 512), bf16),
+            pltpu.VMEM((256, 2048), bf16),
+            pltpu.SemaphoreType.DMA((39,)),
+            pltpu.SemaphoreType.DMA((39,)),
+        ],
+        compiler_params=pltpu.CompilerParams(
+            collective_id=2, has_side_effects=True, vmem_limit_bytes=40 * 1024 * 1024
+        ),
+        name="combine",
+    )(part, weight)
+
+
 def local_kernel(
     steps, code_ref, ks_ref, vs_ref, q_ref, k_ref, v_ref,
-    att_ref, lse_ref,
+    att_ref,
     rows_ref, live_ref, ks0_ref, ks1_ref, vs0_ref, vs1_ref,
     pick_ref, pickt_ref, qs_ref, po_ref, pm_ref, ps_ref,
 ):
@@ -134,7 +509,9 @@
         den = jnp.dot(pickt_ref[...], high, preferred_element_type=f32)
         den = den + jnp.dot(pickt_ref[...], low, preferred_element_type=f32)
         safe = jnp.where(some, den, 1.0)
-        lse_ref[...] = jnp.where(some, shift.astype(f32) + jnp.log2(safe), -1e30)
+        log = pack_log(jnp.where(some, shift.astype(f32) + jnp.log2(safe), -1e30))
+        for start in (0, 1152):
+            att_ref[:, start + 1024 : start + 1152] = log
         ps_ref[...] = factor
         inverse = 1.0 / safe
         for n in range(heads // 2):
@@ -149,7 +526,8 @@
             )
             for j in range(2):
                 h = 2 * n + j
-                att_ref[:, h * 128 : (h + 1) * 128] = (
+                at = h * 128 + 128 * (h // half)
+                att_ref[:, at : at + 128] = (
                     total[:, j * 128 : (j + 1) * 128] * inverse[:, h : h + 1]
                 ).astype(bf16)
 
@@ -164,13 +542,10 @@
     return pl.pallas_call(
         functools.partial(local_kernel, steps),
         grid=(steps,),
-        out_shape=(
-            jax.ShapeDtypeStruct((requests, width), bf16),
-            jax.ShapeDtypeStruct((requests, 128), f32),
-        ),
+        out_shape=jax.ShapeDtypeStruct((requests, width + 256), bf16),
         in_specs=[vmem, vmem, vmem, vmem]
         + [pl.BlockSpec((pages * 32, 128), lambda t: (t, 0))] * 2,
-        out_specs=(vmem, vmem),
+        out_specs=vmem,
         scratch_shapes=[pltpu.VMEM((8, 128), f32)]
         + [pltpu.VMEM((pages, 128), f32)] * 5
         + [
@@ -186,52 +561,6 @@
     )(code, ks, vs, every_query, keys, values)
 
 
-def joined_along(blocks, dim):
-    lengths = list(blocks.shape[1:])
-    lengths[dim] *= blocks.shape[0]
-    return jnp.moveaxis(blocks, 0, dim).reshape(lengths)
-
-
-def from_everyone(shard, axis):
-    copies = jnp.broadcast_to(shard, (lax.axis_size(axis), *shard.shape))
-    return lax.all_to_all(copies, axis, split_axis=0, concat_axis=0, tiled=True)
-
-
-def collect(shard, axis, dim):
-    return joined_along(from_everyone(shard, axis), dim)
-
-
-def split_up(shard, dim, peers):
-    before, after = (shard.shape[:dim], shard.shape[dim + 1 :])
-    return jnp.moveaxis(shard.reshape(*before, peers, -1, *after), dim, 0)
-
-
-def summed_on_arrival(shard, axis, dim):
-    blocks = split_up(shard, dim, lax.axis_size(axis))
-    arrived = lax.all_to_all(blocks, axis, split_axis=0, concat_axis=0, tiled=True)
-    return arrived.astype(jnp.float32).sum(axis=0)
-
-
-def locate_pages(page_table, lengths, pages_here):
-    rows_here, table_width = page_table.shape
-    peers = lax.axis_size("req")
-    entry = jnp.arange(table_width, dtype=jnp.int32)[None, :]
-    live = jnp.clip(lengths[:, None] - 16 * entry, 0, 16)
-    row = jnp.arange(rows_here, dtype=jnp.int32)[:, None]
-    code = jnp.where(live > 0, row * 16 + live, 0).reshape(-1)
-    ids = page_table.reshape(-1)
-    highs = peers * pages_here // 128
-    in_high = (ids[None, :] >> 7) == jnp.arange(highs, dtype=jnp.int32)[:, None]
-    in_low = (ids[:, None] & 127) == jnp.arange(128, dtype=jnp.int32)[None, :]
-    coded = jnp.where(in_low, code[:, None], 0).astype(jnp.bfloat16)
-    blocks = jnp.dot(in_high.astype(jnp.bfloat16), coded, preferred_element_type=jnp.float32)
-    blocks = blocks.reshape(peers, pages_here // 128, 128)
-    found = lax.all_to_all(blocks, "req", split_axis=0, concat_axis=0, tiled=True).astype(jnp.int32)
-    source = jnp.arange(peers, dtype=jnp.int32)[:, None, None]
-    value = jnp.sum(jnp.where(found > 0, source * 256 + found - 1, 0), axis=0)
-    return value.astype(jnp.float32)
-
-
 def on_device(
     queries,
     k_codes,
@@ -242,40 +571,19 @@
     page_table,
     out_weight,
 ):
-    pages_here, page_size, kv_local, head_size = k_codes.shape
-    rows_here, heads_local = queries.shape[:2]
-    sources = lax.axis_size("req")
-    code = locate_pages(page_table, lengths, pages_here)
-    every_query = lax.all_gather(queries.reshape(rows_here, -1), "req", axis=0, tiled=True)
-    part, weight = local_attention(
+    head_size = k_codes.shape[-1]
+    rows_here = queries.shape[0]
+    every_query, code = gather_inputs(lengths, queries.reshape(rows_here, -1), page_table)
+    part = local_attention(
         code,
         key_page_scale.T,
         value_page_scale.T,
-        every_query,
+        every_query.reshape(32 * rows_here, -1),
         k_codes.reshape(-1, head_size),
         value_quantized_codes.reshape(-1, head_size),
     )
-    part_in = lax.all_to_all(
-        part.reshape(sources, rows_here, heads_local * head_size),
-        "req",
-        split_axis=0,
-        concat_axis=0,
-        tiled=True,
-    )
-    weight_in = lax.all_to_all(
-        weight[:, :heads_local].reshape(sources, rows_here, heads_local),
-        "req",
-        split_axis=0,
-        concat_axis=0,
-        tiled=True,
-    )
-    share = jnp.exp2(weight_in - jnp.max(weight_in, axis=0)[None])
-    share = share / jnp.sum(share, axis=0)[None]
-    part_in = part_in.astype(jnp.float32).reshape(sources, rows_here, heads_local, head_size)
-    attention = jnp.sum(part_in * share[..., None], axis=0).reshape(rows_here, -1)
-    attention = attention.astype(jnp.bfloat16)
-    terms = jnp.dot(collect(attention, "req", 0), out_weight, preferred_element_type=jnp.float32)
-    return summed_on_arrival(terms.astype(jnp.bfloat16), "head", 1).astype(jnp.bfloat16)
+    terms = combine(part.reshape(2, 4, 4, rows_here, -1), out_weight)
+    return jnp.sum(terms.astype(jnp.float32), axis=0).astype(jnp.bfloat16).T
 
 
 def solution(mesh):

time: 188 us -> 99.4 us (0.53)
  Pallas kernels: 31.1 us -> 92.7 us
  waiting for transfers between devices: 56.4 us -> 0 us
  blocking collectives: 54.4 us -> 0 us
  between operations: 13.5 us -> 0.04 us
  starting transfers between devices: 12.6 us -> 0 us
  local copies, waits for them, and re-layouts: 11 us -> 5.76 us
  other arithmetic: 5.72 us -> 0.67 us
  matrix products: 2.23 us -> 0 us
    pallas_call x0 -> x2, Pallas kernels: none -> 61.7 us  [the longest x1 41.5 us: combine(): pl.pallas_call(combine_kernel, out_shape=jax.ShapeDtypeStruct((4, 64, 512...]
    all_to_all x3 -> x0, blocking collectives: 54.4 us -> none  [the longest x1 31.8 us: from_everyone(): return lax.all_to_all(copies, axis, split_axis=0, concat_axis=0, tiled=True)]
    all_gather x1 -> x0, waiting for transfers between devices: 29.3 us -> none  [on_device(): lax.all_gather(queries.reshape(rows_here, -1), 'req', axis=0, tiled=True)]
    all_to_all x2 -> x0, waiting for transfers between devices: 27.1 us -> none  [the longest x1 19.4 us: on_device(): lax.all_to_all(part.reshape(sources, rows_here, heads_local * head_size),...]
    all_to_all x2 -> x0, starting transfers between devices: 12.6 us -> none  [the longest x1 8.58 us: locate_pages(): lax.all_to_all(blocks, 'req', split_axis=0, concat_axis=0, tiled=True)]
    mul x2 -> x0, local copies, waits for them, and re-layouts: 7.47 us -> none  [on_device(): part_in * share[..., None]]
    unnamed x5 -> x13, local copies, waits for them, and re-layouts: 2.79 us -> 5.76 us
    reduce_sum x4 -> x1, other arithmetic: 3.52 us -> 0.67 us  [on_device(): return jnp.sum(terms.astype(jnp.float32), axis=0).astype(jnp.bfloat16).T]
  transfers between devices with their start and end apart: 3 -> 0, of which waited for: 3 -> 0; matrix products, arithmetic and copies ran while one was open for 6% -> 0% of each run, Pallas kernels for 0% -> 0%
where the time goes in v3:
time: 99.4 us; the launch traced here: 99.2 us
  Pallas kernels  92.7 us (93%)
  local copies, waits for them, and re-layouts  5.76 us (6%)
    pallas_call x1, Pallas kernels, combine(): pl.pallas_call(combine_kernel, out_shape=jax.ShapeDtypeStruct((4, 64, 512...  41.5 us
    pallas_call x1, Pallas kernels, local_attention(): pl.pallas_call(functools.partial(local_kernel, steps), grid=(steps,), out...  31 us
    pallas_call x1, Pallas kernels, gather_inputs(): pl.pallas_call(gather_kernel, out_shape=(jax.ShapeDtypeStruct((2, 4, 4, r...  20.3 us
    unnamed x13, local copies, waits for them, and re-layouts  5.76 us

profile of v3, /device:TPU:1, one launch (start us, length us, event | category | flops | bytes accessed | tf_op | source)
XLA Modules:
  0.0 99.2 jit_solution(10115031299745702065)
XLA Ops:
  0.0 0.9 copy.11
  0.9 0.0 copy-start.3
  0.9 0.7 copy-done.3
  1.6 0.0 copy-start.5
  1.6 0.7 copy-done.5
  2.2 20.3 %gather_inputs.1 = (bf16[2,4,4,16,2048]{4,3,2,1,0:T(8,128)(2,1)S(1)}, f32[8,128]{1,0:T(8,128)S(1)}) custom-call(s32[16]{0:T(128)S(1)} %copy-done.5, bf16[16,2048]{1,0:T(8,128)(2,1)S(1)} %bitcast.13, s32[16,128]{1,0:T(8,128)S(1)} %copy-done.3), custom_call_target="tpu_custom_call" | custom-call | tf_op jit(solution)/shard_map/gather_inputs/pallas_call | solution.py:181
  22.5 0.0 copy-start.1
  22.5 1.3 %copy-done.1 = bf16[2,4,4,16,2048]{4,3,2,1,0:T(8,128)(2,1)} copy-done((bf16[2,4,4,16,2048]{4,3,2,1,0:T(8,128)(2,1)}, bf16[2,4,4,16,2048]{4,3,2,1,0:T(8,128)(2,1)S(1)}, u32[]{:S(2)}) %copy-start.1) | copy-done | bytes 2097176
  23.8 0.0 copy-start.4
  23.8 0.6 copy-done.4
  24.4 0.0 copy-start.2
  24.4 31.0 %local_attention.1 = bf16[512,2304]{1,0:T(8,128)(2,1)} custom-call(f32[8,128]{1,0:T(8,128)} %copy-done.4, f32[2,1024]{1,0:T(2,128)} %bitcast.17, f32[2,1024]{1,0:T(2,128)} %bitcast.18, bf16[512,2048]{1,0:T(8,128)(2,1)} %bitcast.12, bf16[32768,128]{1,0:T(8,128)(2,1)} %bitcast.14, bf16[32768,128]{1,0:T(8,128)(2,1)} %bitcast.15), custom_call_target="tpu_custom_call" | custom-call | tf_op jit(solution)/shard_map/local_attention/pallas_call | solution.py:542
  55.4 0.0 copy-done.2
  55.4 0.0 copy-start
  55.4 1.7 %copy-done = bf16[512,2304]{1,0:T(8,128)(2,1)S(1)} copy-done((bf16[512,2304]{1,0:T(8,128)(2,1)S(1)}, bf16[512,2304]{1,0:T(8,128)(2,1)}, u32[]{:S(2)}) %copy-start) | copy-done | bytes 2359320
  57.0 41.5 %combine.1 = bf16[4,64,512]{2,1,0:T(8,128)(2,1)S(1)} custom-call(bf16[2,4,4,16,2304]{4,3,2,1,0:T(8,128)(2,1)S(1)} %bitcast.11, bf16[2048,256]{1,0:T(8,128)(2,1)S(1)} %copy-done.2), custom_call_target="tpu_custom_call" | custom-call | tf_op jit(solution)/shard_map/combine/pallas_call | solution.py:361
  98.5 0.7 reduce_sum.12
Async XLA Ops:
  0.9 0.7 copy-start.3
  1.6 0.7 copy-start.5
  22.5 1.3 %copy-start.1 = (bf16[2,4,4,16,2048]{4,3,2,1,0:T(8,128)(2,1)}, bf16[2,4,4,16,2048]{4,3,2,1,0:T(8,128)(2,1)S(1)}, u32[]{:S(2)}) copy-start(bf16[2,4,4,16,2048]{4,3,2,1,0:T(8,128)(2,1)S(1)} %get-tuple-element.8) | copy-start | bytes 6291460
  23.8 0.6 copy-start.4
  24.4 31.0 %copy-start.2 = (bf16[2048,256]{1,0:T(8,128)(2,1)S(1)}, bf16[2048,256]{1,0:T(8,128)(2,1)}, u32[]{:S(2)}) copy-start(bf16[2048,256]{1,0:T(8,128)(2,1)} %weight_ref.1) | copy-start | bytes 3145732
  55.4 1.7 %copy-start = (bf16[512,2304]{1,0:T(8,128)(2,1)S(1)}, bf16[512,2304]{1,0:T(8,128)(2,1)}, u32[]{:S(2)}) copy-start(bf16[512,2304]{1,0:T(8,128)(2,1)} %local_attention.1) | copy-start | bytes 7077892

commit v4 on v3

v4 whole, which is shorter than its diff:
```python
import functools
import math

import jax
import jax.numpy as jnp
from jax import lax
from jax.experimental import pallas as pl
from jax.experimental.pallas import tpu as pltpu
from jax.sharding import PartitionSpec as P

LOG2E = 1.4426950408889634
UNROLL = 8


def pack_log(value):
    f32, bf16 = jnp.float32, jnp.bfloat16
    high = value.astype(bf16).astype(f32)
    middle = (value - high).astype(bf16).astype(f32)
    low = value - high - middle
    lane = lax.broadcasted_iota(jnp.int32, value.shape, 1)
    low = jnp.where(lane < 48, pltpu.roll(low, 32, 1), 0.0)
    low = jnp.where(lane < 32, pltpu.roll(middle, 16, 1), low)
    return jnp.where(lane < 16, high, low).astype(bf16)


def in_two(value):
    f32, bf16 = jnp.float32, jnp.bfloat16
    high = value.astype(bf16).astype(f32)
    lane = lax.broadcasted_iota(jnp.int32, value.shape, 1)
    return jnp.where(lane < 16, high, pltpu.roll(value - high, 16, 1)).astype(bf16)


def of_two(value):
    return value + pltpu.roll(value, 112, 1)


def page_columns(code_ref, ks_ref, vs_ref, rows_ref, wide_ref, pick_ref, pickt_ref):
    f32, bf16 = jnp.float32, jnp.bfloat16
    requests = pickt_ref.shape[0]
    scale = LOG2E / math.sqrt(128.0)

    def body(b, carry):
        code = code_ref[pl.ds(b, 1), :]
        lanes = pl.ds(pl.multiple_of(b * 128, 128), 128)
        owner_row = jnp.floor(code * (1.0 / 16.0))
        rows_ref[0:1, :] = owner_row
        rows_ref[1:2, :] = code - 16.0 * owner_row + 1.0
        rows_ref[2:4, :] = ks_ref[:, lanes] * scale
        rows_ref[4:6, :] = vs_ref[:, lanes]
        cols = rows_ref[...].T
        for i in range(5):
            wide_ref[i, lanes, :] = jnp.broadcast_to(cols[:, i + 1 : i + 2], (128, 128))
        owner = jnp.broadcast_to(cols[:, 0:1], (128, 128))
        lane = lax.broadcasted_iota(jnp.int32, (128, 128), 1).astype(f32)
        for c in range(requests // 128):
            pick_ref[lanes, c * 128 : (c + 1) * 128] = jnp.where(
                owner == lane + float(c * 128), 1.0, 0.0
            ).astype(bf16)
        row = lax.broadcasted_iota(jnp.int32, (requests, 128), 0).astype(f32)
        pickt_ref[:, lanes] = jnp.where(row == owner_row, 1.0, 0.0).astype(bf16)
        return carry

    lax.fori_loop(0, code_ref.shape[0], body, 0)


def page_queries(q_ref, pick_ref, qs_ref):
    f32, bf16 = jnp.float32, jnp.bfloat16
    tiles = qs_ref.shape[0]

    def body(n, carry):
        cols = pl.ds(pl.multiple_of(n * 256, 256), 256)
        queries = q_ref[:, :, :, :, cols].reshape(pick_ref.shape[1], 256)
        got = jnp.dot(pick_ref[...], queries, preferred_element_type=f32)
        pair = [got[:, j * 128 : (j + 1) * 128].reshape(tiles, 8, 128) for j in range(2)]
        qs_ref[:, pl.ds(pl.multiple_of(n * 16, 16), 16), :] = jnp.concatenate(
            pair, axis=1
        ).astype(bf16)
        return carry

    lax.fori_loop(0, q_ref.shape[-1] // 256, body, 0)


def page_sums(k_ref, v_ref, wide_ref, qs_ref, s_ref, p_ref, po_ref, pm_ref, ps_ref):
    f32, bf16 = jnp.float32, jnp.bfloat16
    heads, half = 16, 8
    groups = qs_ref.shape[0] // UNROLL
    lane = lax.broadcasted_iota(jnp.int32, (8, 256), 1)
    sub = lax.broadcasted_iota(jnp.int32, (8, 256), 0)
    own = (lane >> 5) == sub
    token = ((lane & 31) >> 1).astype(f32)
    far = jnp.float32(1e9)
    tokens = [jnp.where(own & ((lane & 1) == j), token, far) for j in range(2)]
    lane8 = lax.broadcasted_iota(jnp.int32, (8, 128), 1)
    ones = jnp.ones((256, 128), bf16)

    def eight(g):
        return pl.ds(pl.multiple_of(g * 8, 8), 8)

    def kv_rows(g):
        return pl.ds(pl.multiple_of(g * 256, 256), 256)

    def values(u, g):
        both = jnp.concatenate([v_ref[kv_rows(g), :], ones], axis=1)
        out = jnp.dot(p_ref[u], both, preferred_element_type=f32)
        ps = jnp.zeros((8, 128), f32)
        for h in range(heads):
            rows = slice(h * 8, h * 8 + 8)
            po_ref[eight(g), h * 128 : (h + 1) * 128] = (
                out[rows, 0:128] * wide_ref[3 + h // half, eight(g), :]
            )
            ps = jnp.where(lane8 == h, out[rows, 128:256], ps)
        ps_ref[eight(g), :] = ps

    def soften(u, g):
        live = wide_ref[0, eight(g), :]
        live = jnp.concatenate([live, live], axis=1)
        pm = jnp.zeros((8, 128), f32)
        for j in range(2):
            keep = (tokens[j] < live)[None]
            scale = wide_ref[1 + j, eight(g), :]
            scale = jnp.concatenate([scale, scale], axis=1)[None]
            part = s_ref[u, j * 64 : (j + 1) * 64, :].reshape(8, 8, 256)
            part = jnp.where(keep, part * scale, -1e30)
            top = jnp.max(part, axis=2, keepdims=True)
            p_ref[u, j * 64 : (j + 1) * 64, :] = (
                jnp.exp2(part - top).reshape(64, 256).astype(bf16)
            )
            for h in range(8):
                pm = jnp.where(lane8 == j * 8 + h, top[h], pm)
        pm_ref[eight(g), :] = pm

    def scores(u, g):
        s_ref[u] = lax.dot_general(
            qs_ref[g], k_ref[kv_rows(g), :], (((1,), (1,)), ((), ())), preferred_element_type=f32
        )

    def body(i, carry):
        for u in range(UNROLL):
            values(u, jnp.maximum(i - 2, 0) * UNROLL + u)
            soften(u, jnp.clip(i - 1, 0, groups - 1) * UNROLL + u)
            scores(u, jnp.minimum(i, groups - 1) * UNROLL + u)
        return carry

    lax.fori_loop(0, groups + 2, body, 0)


def unpack_log(aux):
    aux = aux.astype(jnp.float32)
    return aux + pltpu.roll(aux, 112, 1) + pltpu.roll(aux, 96, 1)


def request_weights(pick_ref, pickt_ref, pm_ref, ps_ref):
    f32, bf16 = jnp.float32, jnp.bfloat16
    pm = pm_ref[...]
    rough = jnp.dot(
        pickt_ref[...], jnp.exp2(pm * (1.0 / 12.0)).astype(bf16), preferred_element_type=f32
    )
    some = rough > 0.0
    shift = jnp.where(some, 12.0 * jnp.log2(jnp.where(some, rough, 1.0)) - 42.0, 0.0).astype(bf16)
    near = pm - jnp.dot(pick_ref[...], shift, preferred_element_type=f32)
    den = of_two(
        jnp.dot(pickt_ref[...], in_two(ps_ref[...] * jnp.exp2(near)), preferred_element_type=f32)
    )
    log = shift.astype(f32) + jnp.log2(jnp.where(some, den, 1.0))
    log = pack_log(jnp.where(some, log, -1e30))
    back = unpack_log(jnp.dot(pick_ref[...], log, preferred_element_type=f32))
    ps_ref[...] = jnp.exp2(jnp.minimum(pm - back, 64.0))
    return log


def request_sums(n, pickt_ref, po_ref, ps_ref):
    f32, bf16 = jnp.float32, jnp.bfloat16
    cols = [
        (po_ref[:, h * 128 : (h + 1) * 128] * ps_ref[:, h : h + 1]).astype(bf16)
        for h in (2 * n, 2 * n + 1)
    ]
    return jnp.dot(
        pickt_ref[...], jnp.concatenate(cols, axis=1), preferred_element_type=f32
    ).astype(bf16)


MESH = pl.DeviceIdType.MESH


def place():
    me = lax.axis_index("req")
    return lax.div(me, 8), lax.rem(lax.div(me, 2), 4), lax.rem(me, 2)


def off(i, d):
    return lax.rem(i + d + 4, 4)


def chip(x, y, c):
    return {"req": (x * 4 + y) * 2 + c}


class Copies:
    def __init__(self, send_sems, recv_sems):
        self.sems, self.count, self.sent = (send_sems, recv_sems), 0, []

    def send(self, source, target, device, landing):
        pair = (self.sems[0].at[self.count], self.sems[1].at[self.count])
        self.count += 1
        copy = pltpu.make_async_remote_copy(source, target, *pair, device, device_id_type=MESH)
        copy.start()
        self.sent.append(copy)
        return pltpu.make_async_remote_copy(source, landing, *pair, device, device_id_type=MESH)

    def drain(self):
        for copy in self.sent:
            copy.wait_send()


def greet(x, y, c, others=()):
    barrier = pltpu.get_barrier_semaphore()
    peers = [chip(off(x, d), y, c) for d in (1, 2, 3)]
    peers += [chip(x, off(y, d), c) for d in (1, 2, 3)]
    peers += [chip(x, y, 1 - c)] + list(others)
    for peer in peers:
        pl.semaphore_signal(barrier, inc=1, device_id=peer, device_id_type=MESH)
    pl.semaphore_wait(barrier, len(peers))


def gather_first(copies, own, view, x, y, c, halves):
    left, right = halves
    waits = []
    for d in (2, 1, 3):
        waits.append(
            copies.send(
                own.at[:, left], view(x, y, c, left), chip(x, off(y, d), c),
                view(x, off(y, -d), c, left),
            )
        )
        waits.append(
            copies.send(
                own.at[:, right], view(x, y, c, right), chip(off(x, d), y, c),
                view(off(x, -d), y, c, right),
            )
        )
    return waits


def gather_second(copies, view, x, y, c, halves):
    left, right = halves
    every = slice(None)
    waits = []
    for d in (2, 1, 3):
        waits.append(
            copies.send(
                view(x, every, c, left), view(x, every, c, left), chip(off(x, d), y, c),
                view(off(x, -d), every, c, left),
            )
        )
        waits.append(
            copies.send(
                view(every, y, c, right), view(every, y, c, right), chip(x, off(y, d), c),
                view(every, off(y, -d), c, right),
            )
        )
    return waits


def gather_third(copies, waits, view, x, y, c, halves):
    left, right = halves
    every = slice(None)
    twin = chip(x, y, 1 - c)
    last = []

    def pass_on(piece, theirs):
        last.append(copies.send(piece, piece, twin, theirs))

    pass_on(view(x, every, c, left), view(x, every, 1 - c, left))
    pass_on(view(every, y, c, right), view(every, y, 1 - c, right))
    for k, d in enumerate((2, 1, 3)):
        waits[2 * k].wait_recv()
        row = off(x, -d)
        pass_on(view(row, every, c, left), view(row, every, 1 - c, left))
        waits[2 * k + 1].wait_recv()
        row = off(y, -d)
        pass_on(view(every, row, c, right), view(every, row, 1 - c, right))
    return last


def merged(blocks, first_head):
    logs = [unpack_log(b[:, 1024:1152]) for b in blocks]
    top = functools.reduce(jnp.maximum, logs)
    shares = [jnp.exp2(g - top) for g in logs]
    total = functools.reduce(jnp.add, shares)
    inverse = 1.0 / total
    shares = [s * inverse for s in shares]
    columns = []
    for h in range(8):
        at = first_head + h
        columns.append(
            functools.reduce(
                jnp.add,
                [
                    b[:, h * 128 : (h + 1) * 128].astype(jnp.float32) * s[:, at : at + 1]
                    for b, s in zip(blocks, shares)
                ],
            ).astype(jnp.bfloat16)
        )
    return columns, top + jnp.log2(total)


def store_merged(target, index, start, blocks, first_head):
    columns, log = merged(blocks, first_head)
    for h, column in enumerate(columns):
        target[index + (slice(None), slice(start + h * 128, start + (h + 1) * 128))] = column
    if target.shape[-1] != 2048:
        target[index + (slice(None), slice(start + 1024, start + 1152))] = pack_log(log)


def whole_kernel(
    lengths_ref, q_ref, table_ref, ks_ref, vs_ref, k_hbm, v_hbm, weight_ref, out_ref,
    k_ref, v_ref, every_ref, code_ref, table_out, sum_y, sum_c, in_x, in_y, in_c,
    rows_ref, wide_ref, pick_ref, pickt_ref, qs_ref, s_ref, p_ref, po_ref, pm_ref, ps_ref,
    part_ref, twin_in, now, in_left, in_right, left_now, right_now, in_left2, in_right2,
    own, all_ref, terms, turned, load_sems, send_sems, recv_sems,
):
    f32, bf16 = jnp.float32, jnp.bfloat16
    x, y, c = place()
    z = lax.axis_index("head")
    every = slice(None)
    wide = 1152
    left, right = slice(0, wide), slice(wide, 2 * wide)
    rows, width = q_ref.shape
    halves = (slice(0, width // 2), slice(width // 2, width))
    loads = [
        pltpu.make_async_copy(k_hbm, k_ref, load_sems.at[0]),
        pltpu.make_async_copy(v_hbm, v_ref, load_sems.at[1]),
    ]
    for load in loads:
        load.start()

    def view_all(i, j, k, cols):
        return every_ref.at[k, i, j, :, cols]

    greet(x, y, c, [{"head": off(z, d)} for d in (1, 2, 3)])
    copies = Copies(send_sems, recv_sems)
    first = gather_first(copies, q_ref, view_all, x, y, c, halves)
    every_ref[c, x, y] = q_ref[...]
    lane = lax.broadcasted_iota(jnp.int32, (1, 128), 1)
    high_id = lax.broadcasted_iota(jnp.int32, (256, 128), 0)
    low_id = lax.broadcasted_iota(jnp.int32, (128, 128), 0)
    highs, lows = [], []
    for r in range(rows):
        live = jnp.clip(lengths_ref[r] - 16 * lane, 0, 16)
        coded = jnp.where(live > 0, live + 16 * r, 0).astype(f32)
        ids = table_ref[r : r + 1, :]
        highs.append(jnp.where(high_id == (ids >> 7), 1.0, 0.0).astype(bf16))
        lows.append(jnp.where(low_id == (ids & 127), coded, 0.0).astype(bf16))
    found = lax.dot_general(
        jnp.concatenate(highs, axis=1), jnp.concatenate(lows, axis=1),
        (((1,), (1,)), ((), ())), preferred_element_type=f32,
    )
    base = ((c * 16 + x * 4 + y) * 256).astype(f32)
    table_out[...] = jnp.where(found > 0.0, found + base, 0.0).reshape(4, 4, 2, 8, 128)
    got = [
        copies.send(
            table_out.at[off(x, d)], in_x.at[d - 1], chip(off(x, d), y, c), in_x.at[d - 1]
        )
        for d in (2, 1, 3)
    ]
    for wait in first:
        wait.wait_recv()
    second = gather_second(copies, view_all, x, y, c, halves)
    for wait in got:
        wait.wait_recv()
    sum_y[...] = table_out[x] + in_x[0] + in_x[1] + in_x[2]
    got = [
        copies.send(sum_y.at[off(y, d)], in_y.at[d - 1], chip(x, off(y, d), c), in_y.at[d - 1])
        for d in (2, 1, 3)
    ]
    for wait in got:
        wait.wait_recv()
    sum_c[...] = sum_y[y] + in_y[0] + in_y[1] + in_y[2]
    got = copies.send(sum_c.at[1 - c], in_c, chip(x, y, 1 - c), in_c)
    got.wait_recv()
    code_ref[...] = sum_c[c] + in_c[...] - 1.0
    page_columns(code_ref, ks_ref, vs_ref, rows_ref, wide_ref, pick_ref, pickt_ref)
    for k in range(16):
        turned[:, k * 128 : (k + 1) * 128] = weight_ref[k * 128 : (k + 1) * 128, :].T
    for wait in gather_third(copies, second, view_all, x, y, c, halves):
        wait.wait_recv()
    page_queries(every_ref, pick_ref, qs_ref)
    for load in loads:
        load.wait()
    page_sums(k_ref, v_ref, wide_ref, qs_ref, s_ref, p_ref, po_ref, pm_ref, ps_ref)
    log = request_weights(pick_ref, pickt_ref, pm_ref, ps_ref).reshape(2, 4, 4, rows, 128)
    part_ref[:, :, :, :, 1024:1152] = log
    part_ref[:, :, :, :, 1152 + 1024 :] = log
    for n in range(8):
        at = n * 256 + 128 * (n // 4)
        part_ref[:, :, :, :, at : at + 256] = request_sums(
            n, pickt_ref, po_ref, ps_ref
        ).reshape(2, 4, 4, rows, 256)


    twin = [
        copies.send(part_ref.at[1 - c, i], twin_in.at[i], chip(x, y, 1 - c), twin_in.at[i])
        for i in range(4)
    ]
    for i in range(4):
        twin[i].wait_recv()

        def body(j, carry):
            for start, head in ((0, 0), (wide, 8)):
                cols = slice(start, start + wide)
                store_merged(
                    now, (i, j), start, [part_ref[c, i, j, :, cols], twin_in[i, j, :, cols]], head
                )
            return carry

        lax.fori_loop(0, 4, body, 0)
    waits = []
    for d in (2, 1, 3):
        waits.append(
            copies.send(
                now.at[off(x, d), :, :, left], in_left.at[d - 1], chip(off(x, d), y, c),
                in_left.at[d - 1],
            )
        )
        waits.append(
            copies.send(
                now.at[:, off(y, d), :, right], in_right.at[d - 1], chip(x, off(y, d), c),
                in_right.at[d - 1],
            )
        )
    for wait in waits:
        wait.wait_recv()

    def body(j, carry):
        store_merged(
            left_now, (j,), 0, [now[x, j, :, left]] + [in_left[d, j] for d in range(3)], 0
        )
        store_merged(
            right_now, (j,), 0, [now[j, y, :, right]] + [in_right[d, j] for d in range(3)], 8
        )
        return carry

    lax.fori_loop(0, 4, body, 0)
    waits = []
    for d in (2, 1, 3):
        waits.append(
            copies.send(
                left_now.at[off(y, d)], in_left2.at[d - 1], chip(x, off(y, d), c),
                in_left2.at[d - 1],
            )
        )
        waits.append(
            copies.send(
                right_now.at[off(x, d)], in_right2.at[d - 1], chip(off(x, d), y, c),
                in_right2.at[d - 1],
            )
        )
    for wait in waits:
        wait.wait_recv()
    store_merged(own, (), 0, [left_now[y]] + [in_left2[d] for d in range(3)], 0)
    store_merged(own, (), 1024, [right_now[x]] + [in_right2[d] for d in range(3)], 8)

    def view(i, j, k, cols):
        return all_ref.at[i, j, k, :, cols]

    first = gather_first(copies, own, view, x, y, c, halves)
    all_ref[x, y, c] = own[...]
    for wait in first:
        wait.wait_recv()
    second = gather_second(copies, view, x, y, c, halves)
    for wait in gather_third(copies, second, view, x, y, c, halves):
        wait.wait_recv()
    attention = all_ref[...].reshape(512, 2048)
    terms[...] = (
        lax.dot_general(
            turned[...], attention, (((1,), (1,)), ((), ())), preferred_element_type=f32
        )
        .astype(bf16)
        .reshape(4, 64, 512)
    )
    waits = [
        copies.send(terms.at[off(z, d)], out_ref.at[d], {"head": off(z, d)}, out_ref.at[d])
        for d in (2, 1, 3)
    ]
    out_ref[0] = terms[z]
    for wait in waits:
        wait.wait_recv()
    copies.drain()


def whole(lengths, queries, page_table, ks, vs, keys, values, weight):
    f32, bf16 = jnp.float32, jnp.bfloat16
    rows, width = queries.shape
    pages = keys.shape[0] // 32
    requests = 32 * rows
    vmem = pl.BlockSpec(memory_space=pltpu.VMEM)
    hbm = pl.BlockSpec(memory_space=pl.ANY)
    return pl.pallas_call(
        whole_kernel,
        out_shape=jax.ShapeDtypeStruct((4, 64, 512), bf16),
        in_specs=[pl.BlockSpec(memory_space=pltpu.SMEM), vmem, vmem, vmem, vmem, hbm, hbm, vmem],
        out_specs=vmem,
        scratch_shapes=[
            pltpu.VMEM(keys.shape, bf16),
            pltpu.VMEM(keys.shape, bf16),
            pltpu.VMEM((2, 4, 4, rows, width), bf16),
            pltpu.VMEM((8, 128), f32),
            pltpu.VMEM((4, 4, 2, 8, 128), f32),
            pltpu.VMEM((4, 2, 8, 128), f32),
            pltpu.VMEM((2, 8, 128), f32),
            pltpu.VMEM((3, 4, 2, 8, 128), f32),
            pltpu.VMEM((3, 2, 8, 128), f32),
            pltpu.VMEM((8, 128), f32),
            pltpu.VMEM((8, 128), f32),
            pltpu.VMEM((5, pages, 128), f32),
            pltpu.VMEM((pages, requests), bf16),
            pltpu.VMEM((requests, pages), bf16),
            pltpu.VMEM((pages // 8, 128, 128), bf16),
            pltpu.VMEM((UNROLL, 128, 256), f32),
            pltpu.VMEM((UNROLL, 128, 256), bf16),
            pltpu.VMEM((pages, width), f32),
            pltpu.VMEM((pages, 128), f32),
            pltpu.VMEM((pages, 128), f32),
            pltpu.VMEM((2, 4, 4, 16, 2304), bf16),
            pltpu.VMEM((4, 4, 16, 2304), bf16),
            pltpu.VMEM((4, 4, 16, 2304), bf16),
            pltpu.VMEM((3, 4, 16, 1152), bf16),
            pltpu.VMEM((3, 4, 16, 1152), bf16),
            pltpu.VMEM((4, 16, 1152), bf16),
            pltpu.VMEM((4, 16, 1152), bf16),
            pltpu.VMEM((3, 16, 1152), bf16),
            pltpu.VMEM((3, 16, 1152), bf16),
            pltpu.VMEM((16, 2048), bf16),
            pltpu.VMEM((4, 4, 2, 16, 2048), bf16),
            pltpu.VMEM((4, 64, 512), bf16),
            pltpu.VMEM((256, 2048), bf16),
            pltpu.SemaphoreType.DMA((2,)),
            pltpu.SemaphoreType.DMA((66,)),
            pltpu.SemaphoreType.DMA((66,)),
        ],
        compiler_params=pltpu.CompilerParams(
            collective_id=1, has_side_effects=True, vmem_limit_bytes=60 * 1024 * 1024
        ),
        name="whole",
    )(lengths, queries, page_table, ks, vs, keys, values, weight)


def on_device(
    queries,
    k_codes,
    value_quantized_codes,
    key_page_scale,
    value_page_scale,
    lengths,
    page_table,
    out_weight,
):
    head_size = k_codes.shape[-1]
    terms = whole(
        lengths,
        queries.reshape(queries.shape[0], -1),
        page_table,
        key_page_scale.T,
        value_page_scale.T,
        k_codes.reshape(-1, head_size),
        value_quantized_codes.reshape(-1, head_size),
        out_weight,
    )
    return jnp.sum(terms.astype(jnp.float32), axis=0).astype(jnp.bfloat16).T


def solution(mesh):
    in_specs = (
        P("req", "head", None),
        P("req", None, "head", None),
        P("req", None, "head", None),
        P("req", "head"),
        P("req", "head"),
        P("req"),
        P("req", None),
        P("head", "req"),
    )
    out_specs = P(None, ("req", "head"))
    return jax.shard_map(
        on_device, mesh=mesh, in_specs=in_specs, out_specs=out_specs, check_vma=False
    )
```

time: 99.4 us -> 88.5 us (0.89)
  Pallas kernels: 92.7 us -> 85.2 us
  local copies, waits for them, and re-layouts: 5.76 us -> 1.49 us
    pallas_call x3 -> x1, Pallas kernels: 92.7 us -> 85.2 us  [whole(): pl.pallas_call(whole_kernel, out_shape=jax.ShapeDtypeStruct((4, 64, 512),...]
    unnamed x13 -> x1, local copies, waits for them, and re-layouts: 5.76 us -> 1.49 us
where the time goes in v4:
time: 88.5 us; the launch traced here: 88.3 us
  Pallas kernels  85.2 us (96%)
  other arithmetic  1.64 us (2%)
  local copies, waits for them, and re-layouts  1.49 us (2%)
    pallas_call x1, Pallas kernels, whole(): pl.pallas_call(whole_kernel, out_shape=jax.ShapeDtypeStruct((4, 64, 512),...  85.2 us

profile of v4, /device:TPU:1, one launch (start us, length us, event | category | flops | bytes accessed | tf_op | source)
XLA Modules:
  0.0 88.3 jit_solution(13621019904682218386)
XLA Ops:
  0.0 1.5 %copy.11 = bf16[2,8,16,128]{3,1,2,0:T(8,128)(2,1)} copy(bf16[2,8,16,128]{3,2,1,0:T(8,128)(2,1)} %bitcast.12) | data formatting | bytes 131072
  1.5 85.2 %whole.1 = bf16[4,64,512]{2,1,0:T(8,128)(2,1)} custom-call(s32[16]{0:T(128)} %lengths_ref.1, bf16[16,2048]{1,0:T(8,128)(2,1)} %bitcast.11, s32[16,128]{1,0:T(8,128)} %table_ref.1, f32[2,1024]{1,0:T(2,128)} %bitcast.13, f32[2,1024]{1,0:T(2,128)} %bitcast.14, bf16[32768,128]{1,0:T(8,128)(2,1)} %bitcast.9, bf16[32768,128]{1,0:T(8,128)(2,1)} %bitcast.10, ...), custom_call_target="tpu_custom_call" | custom-call | tf_op jit(solution)/shard_map/whole/pallas_call | solution.py:498
  86.7 1.6 %reduce_sum.12 = bf16[64,512]{1,0:T(8,128)(2,1)} reduce(bf16[4,64,512]{2,1,0:T(8,128)(2,1)} %whole.1, bf16[]{:T(256)} %constant.2.clone.1), dimensions={0}, to_apply=%region_0.0 | reduce | flops 98304 | bytes 327682 | tf_op jit(solution)/shard_map/reduce_sum | solution.py:569

commit v5 on v4

--- a/solution.py
+++ b/solution.py
@@ -212,14 +212,11 @@
             copy.wait_send()
 
 
-def greet(x, y, c, others=()):
+def greet(peers):
     barrier = pltpu.get_barrier_semaphore()
-    peers = [chip(off(x, d), y, c) for d in (1, 2, 3)]
-    peers += [chip(x, off(y, d), c) for d in (1, 2, 3)]
-    peers += [chip(x, y, 1 - c)] + list(others)
     for peer in peers:
         pl.semaphore_signal(barrier, inc=1, device_id=peer, device_id_type=MESH)
-    pl.semaphore_wait(barrier, len(peers))
+    return lambda: pl.semaphore_wait(barrier, len(peers))
 
 
 def gather_first(copies, own, view, x, y, c, halves):
@@ -261,72 +258,70 @@
     return waits
 
 
-def gather_third(copies, waits, view, x, y, c, halves):
+def pass_own(copies, view, x, y, c, halves):
+    left, right = halves
+    every = slice(None)
+    twin = chip(x, y, 1 - c)
+    return [
+        copies.send(view(x, every, c, left), view(x, every, c, left), twin,
+                    view(x, every, 1 - c, left)),
+        copies.send(view(every, y, c, right), view(every, y, c, right), twin,
+                    view(every, y, 1 - c, right)),
+    ]
+
+
+def pass_on(copies, waits, view, x, y, c, halves):
     left, right = halves
     every = slice(None)
     twin = chip(x, y, 1 - c)
     last = []
-
-    def pass_on(piece, theirs):
-        last.append(copies.send(piece, piece, twin, theirs))
-
-    pass_on(view(x, every, c, left), view(x, every, 1 - c, left))
-    pass_on(view(every, y, c, right), view(every, y, 1 - c, right))
     for k, d in enumerate((2, 1, 3)):
         waits[2 * k].wait_recv()
-        row = off(x, -d)
-        pass_on(view(row, every, c, left), view(row, every, 1 - c, left))
+        i = off(x, -d)
+        piece = view(i, every, c, left)
+        last.append(copies.send(piece, piece, twin, view(i, every, 1 - c, left)))
         waits[2 * k + 1].wait_recv()
-        row = off(y, -d)
-        pass_on(view(every, row, c, right), view(every, row, 1 - c, right))
+        j = off(y, -d)
+        piece = view(every, j, c, right)
+        last.append(copies.send(piece, piece, twin, view(every, j, 1 - c, right)))
     return last
 
 
-def merged(blocks, first_head):
-    logs = [unpack_log(b[:, 1024:1152]) for b in blocks]
+def wait_all(waits):
+    for wait in waits:
+        wait.wait_recv()
+
+
+def shares_of(logs):
     top = functools.reduce(jnp.maximum, logs)
     shares = [jnp.exp2(g - top) for g in logs]
     total = functools.reduce(jnp.add, shares)
     inverse = 1.0 / total
-    shares = [s * inverse for s in shares]
-    columns = []
-    for h in range(8):
-        at = first_head + h
-        columns.append(
-            functools.reduce(
-                jnp.add,
-                [
-                    b[:, h * 128 : (h + 1) * 128].astype(jnp.float32) * s[:, at : at + 1]
-                    for b, s in zip(blocks, shares)
-                ],
-            ).astype(jnp.bfloat16)
-        )
-    return columns, top + jnp.log2(total)
-
-
-def store_merged(target, index, start, blocks, first_head):
-    columns, log = merged(blocks, first_head)
-    for h, column in enumerate(columns):
-        target[index + (slice(None), slice(start + h * 128, start + (h + 1) * 128))] = column
-    if target.shape[-1] != 2048:
-        target[index + (slice(None), slice(start + 1024, start + 1152))] = pack_log(log)
+    return [s * inverse for s in shares], pack_log(top + jnp.log2(total))
+
+
+def blended(blocks, shares, head):
+    terms = [b.astype(jnp.float32) * s[:, head : head + 1] for b, s in zip(blocks, shares)]
+    return functools.reduce(jnp.add, terms).astype(jnp.bfloat16)
 
 
 def whole_kernel(
     lengths_ref, q_ref, table_ref, ks_ref, vs_ref, k_hbm, v_hbm, weight_ref, out_ref,
     k_ref, v_ref, every_ref, code_ref, table_out, sum_y, sum_c, in_x, in_y, in_c,
     rows_ref, wide_ref, pick_ref, pickt_ref, qs_ref, s_ref, p_ref, po_ref, pm_ref, ps_ref,
-    part_ref, twin_in, now, in_left, in_right, left_now, right_now, in_left2, in_right2,
+    part_ref, log_ref, twin_in, log_in, now, now_log, share0,
+    in_left, in_right, log_left, log_right, share_left, share_right,
+    left_now, right_now, left_log, right_log,
+    in_left2, in_right2, log_left2, log_right2, share_left2, share_right2,
     own, all_ref, terms, turned, load_sems, send_sems, recv_sems,
 ):
     f32, bf16 = jnp.float32, jnp.bfloat16
     x, y, c = place()
     z = lax.axis_index("head")
-    every = slice(None)
-    wide = 1152
-    left, right = slice(0, wide), slice(wide, 2 * wide)
     rows, width = q_ref.shape
-    halves = (slice(0, width // 2), slice(width // 2, width))
+    chunks = [
+        (slice(k * 512, k * 512 + 512), slice(1024 + k * 512, 1536 + k * 512)) for k in range(2)
+    ]
     loads = [
         pltpu.make_async_copy(k_hbm, k_ref, load_sems.at[0]),
         pltpu.make_async_copy(v_hbm, v_ref, load_sems.at[1]),
@@ -337,10 +332,11 @@
     def view_all(i, j, k, cols):
         return every_ref.at[k, i, j, :, cols]
 
-    greet(x, y, c, [{"head": off(z, d)} for d in (1, 2, 3)])
+    peers = [chip(off(x, d), y, c) for d in (1, 2, 3)]
+    peers += [chip(x, off(y, d), c) for d in (1, 2, 3)]
+    peers += [chip(x, y, 1 - c)] + [{"head": off(z, d)} for d in (1, 2, 3)]
+    met = greet(peers)
     copies = Copies(send_sems, recv_sems)
-    first = gather_first(copies, q_ref, view_all, x, y, c, halves)
-    every_ref[c, x, y] = q_ref[...]
     lane = lax.broadcasted_iota(jnp.int32, (1, 128), 1)
     high_id = lax.broadcasted_iota(jnp.int32, (256, 128), 0)
     low_id = lax.broadcasted_iota(jnp.int32, (128, 128), 0)
@@ -357,119 +353,213 @@
     )
     base = ((c * 16 + x * 4 + y) * 256).astype(f32)
     table_out[...] = jnp.where(found > 0.0, found + base, 0.0).reshape(4, 4, 2, 8, 128)
+    every_ref[c, x, y] = q_ref[...]
+    met()
     got = [
         copies.send(
             table_out.at[off(x, d)], in_x.at[d - 1], chip(off(x, d), y, c), in_x.at[d - 1]
         )
         for d in (2, 1, 3)
     ]
-    for wait in first:
-        wait.wait_recv()
-    second = gather_second(copies, view_all, x, y, c, halves)
-    for wait in got:
-        wait.wait_recv()
+    first = [gather_first(copies, q_ref, view_all, x, y, c, halves) for halves in chunks]
+    wait_all(got)
     sum_y[...] = table_out[x] + in_x[0] + in_x[1] + in_x[2]
     got = [
         copies.send(sum_y.at[off(y, d)], in_y.at[d - 1], chip(x, off(y, d), c), in_y.at[d - 1])
         for d in (2, 1, 3)
     ]
-    for wait in got:
-        wait.wait_recv()
+    second, third = [], []
+    for halves, waits in zip(chunks, first):
+        wait_all(waits)
+        second.append(gather_second(copies, view_all, x, y, c, halves))
+        third += pass_own(copies, view_all, x, y, c, halves)
+    wait_all(got)
     sum_c[...] = sum_y[y] + in_y[0] + in_y[1] + in_y[2]
-    got = copies.send(sum_c.at[1 - c], in_c, chip(x, y, 1 - c), in_c)
-    got.wait_recv()
+    copies.send(sum_c.at[1 - c], in_c, chip(x, y, 1 - c), in_c).wait_recv()
     code_ref[...] = sum_c[c] + in_c[...] - 1.0
     page_columns(code_ref, ks_ref, vs_ref, rows_ref, wide_ref, pick_ref, pickt_ref)
     for k in range(16):
         turned[:, k * 128 : (k + 1) * 128] = weight_ref[k * 128 : (k + 1) * 128, :].T
-    for wait in gather_third(copies, second, view_all, x, y, c, halves):
-        wait.wait_recv()
+    for halves, waits in zip(chunks, second):
+        third += pass_on(copies, waits, view_all, x, y, c, halves)
+    wait_all(third)
     page_queries(every_ref, pick_ref, qs_ref)
     for load in loads:
         load.wait()
     page_sums(k_ref, v_ref, wide_ref, qs_ref, s_ref, p_ref, po_ref, pm_ref, ps_ref)
-    log = request_weights(pick_ref, pickt_ref, pm_ref, ps_ref).reshape(2, 4, 4, rows, 128)
-    part_ref[:, :, :, :, 1024:1152] = log
-    part_ref[:, :, :, :, 1152 + 1024 :] = log
-    for n in range(8):
-        at = n * 256 + 128 * (n // 4)
-        part_ref[:, :, :, :, at : at + 256] = request_sums(
-            n, pickt_ref, po_ref, ps_ref
-        ).reshape(2, 4, 4, rows, 256)
-
-
-    twin = [
-        copies.send(part_ref.at[1 - c, i], twin_in.at[i], chip(x, y, 1 - c), twin_in.at[i])
-        for i in range(4)
-    ]
-    for i in range(4):
-        twin[i].wait_recv()
+    log_ref[...] = request_weights(pick_ref, pickt_ref, pm_ref, ps_ref).reshape(
+        2, 4, 4, rows, 128
+    )
+    twin = chip(x, y, 1 - c)
+    log_wait = copies.send(log_ref.at[1 - c], log_in, twin, log_in)
+
+    def sums(*pairs):
+        for n in pairs:
+            part_ref[:, :, :, :, n * 256 : n * 256 + 256] = request_sums(
+                n, pickt_ref, po_ref, ps_ref
+            ).reshape(2, 4, 4, rows, 256)
+
+    def to_twin(halves):
+        return [
+            copies.send(
+                part_ref.at[1 - c, :, :, :, cols], twin_in.at[:, :, :, cols], twin,
+                twin_in.at[:, :, :, cols],
+            )
+            for cols in halves
+        ]
+
+    def first_shares(j, carry):
+        for i in range(4):
+            shares, log = shares_of([unpack_log(log_ref[c, i, j]), unpack_log(log_in[i, j])])
+            now_log[i, j] = log
+            for k in range(2):
+                share0[k, i, j] = shares[k]
+        return carry
+
+    def across(k, waits):
+        wait_all(waits)
+
+        def body(i, carry):
+            for j in range(4):
+                shares = [share0[0, i, j], share0[1, i, j]]
+                for h in range(4):
+                    for side in range(2):
+                        at = side * 1024 + k * 512 + h * 128
+                        cols = slice(at, at + 128)
+                        now[i, j, :, cols] = blended(
+                            [part_ref[c, i, j, :, cols], twin_in[i, j, :, cols]],
+                            shares, side * 8 + k * 4 + h,
+                        )
+            return carry
+
+        lax.fori_loop(0, 4, body, 0)
+        left, right = chunks[k]
+        near = chunks[k][0]
+        waits, logs = [], []
+        for d in (2, 1, 3):
+            to_x, to_y = chip(off(x, d), y, c), chip(x, off(y, d), c)
+            if k == 0:
+                logs.append(
+                    copies.send(
+                        now_log.at[off(x, d)], log_left.at[d - 1], to_x, log_left.at[d - 1]
+                    )
+                )
+                logs.append(
+                    copies.send(
+                        now_log.at[:, off(y, d)], log_right.at[d - 1], to_y, log_right.at[d - 1]
+                    )
+                )
+            here = in_left.at[d - 1, :, :, near]
+            waits.append(copies.send(now.at[off(x, d), :, :, left], here, to_x, here))
+            here = in_right.at[d - 1, :, :, near]
+            waits.append(copies.send(now.at[:, off(y, d), :, right], here, to_y, here))
+        return waits, logs
+
+    def second_shares(j, carry):
+        logs = [now_log[x, j]] + [log_left[d, j] for d in range(3)]
+        shares, log = shares_of([unpack_log(g) for g in logs])
+        left_log[j] = log
+        for k in range(4):
+            share_left[k, j] = shares[k]
+        logs = [now_log[j, y]] + [log_right[d, j] for d in range(3)]
+        shares, log = shares_of([unpack_log(g) for g in logs])
+        right_log[j] = log
+        for k in range(4):
+            share_right[k, j] = shares[k]
+        return carry
+
+    def along(k, waits):
+        wait_all(waits)
 
         def body(j, carry):
-            for start, head in ((0, 0), (wide, 8)):
-                cols = slice(start, start + wide)
-                store_merged(
-                    now, (i, j), start, [part_ref[c, i, j, :, cols], twin_in[i, j, :, cols]], head
+            shares = [share_left[i, j] for i in range(4)]
+            for h in range(4):
+                at = k * 512 + h * 128
+                cols = slice(at, at + 128)
+                blocks = [now[x, j, :, cols]] + [in_left[d, j, :, cols] for d in range(3)]
+                left_now[j, :, cols] = blended(blocks, shares, k * 4 + h)
+            shares = [share_right[i, j] for i in range(4)]
+            for h in range(4):
+                at = k * 512 + h * 128
+                cols = slice(at, at + 128)
+                blocks = [now[j, y, :, 1024 + at : 1152 + at]]
+                blocks += [in_right[d, j, :, cols] for d in range(3)]
+                right_now[j, :, cols] = blended(blocks, shares, 8 + k * 4 + h)
+            return carry
+
+        lax.fori_loop(0, 4, body, 0)
+        near = chunks[k][0]
+        waits, logs = [], []
+        for d in (2, 1, 3):
+            to_x, to_y = chip(off(x, d), y, c), chip(x, off(y, d), c)
+            if k == 0:
+                logs.append(
+                    copies.send(
+                        left_log.at[off(y, d)], log_left2.at[d - 1], to_y, log_left2.at[d - 1]
+                    )
                 )
-            return carry
-
-        lax.fori_loop(0, 4, body, 0)
-    waits = []
-    for d in (2, 1, 3):
-        waits.append(
-            copies.send(
-                now.at[off(x, d), :, :, left], in_left.at[d - 1], chip(off(x, d), y, c),
-                in_left.at[d - 1],
-            )
-        )
-        waits.append(
-            copies.send(
-                now.at[:, off(y, d), :, right], in_right.at[d - 1], chip(x, off(y, d), c),
-                in_right.at[d - 1],
-            )
-        )
-    for wait in waits:
-        wait.wait_recv()
-
-    def body(j, carry):
-        store_merged(
-            left_now, (j,), 0, [now[x, j, :, left]] + [in_left[d, j] for d in range(3)], 0
-        )
-        store_merged(
-            right_now, (j,), 0, [now[j, y, :, right]] + [in_right[d, j] for d in range(3)], 8
-        )
-        return carry
-
-    lax.fori_loop(0, 4, body, 0)
-    waits = []
-    for d in (2, 1, 3):
-        waits.append(
-            copies.send(
-                left_now.at[off(y, d)], in_left2.at[d - 1], chip(x, off(y, d), c),
-                in_left2.at[d - 1],
-            )
-        )
-        waits.append(
-            copies.send(
-                right_now.at[off(x, d)], in_right2.at[d - 1], chip(off(x, d), y, c),
-                in_right2.at[d - 1],
-            )
-        )
-    for wait in waits:
-        wait.wait_recv()
-    store_merged(own, (), 0, [left_now[y]] + [in_left2[d] for d in range(3)], 0)
-    store_merged(own, (), 1024, [right_now[x]] + [in_right2[d] for d in range(3)], 8)
+                logs.append(
+                    copies.send(
+                        right_log.at[off(x, d)], log_right2.at[d - 1], to_x, log_right2.at[d - 1]
+                    )
+                )
+            here = in_left2.at[d - 1, :, near]
+            waits.append(copies.send(left_now.at[off(y, d), :, near], here, to_y, here))
+            here = in_right2.at[d - 1, :, near]
+            waits.append(copies.send(right_now.at[off(x, d), :, near], here, to_x, here))
+        return waits, logs
+
+    def third_shares():
+        logs = [left_log[y]] + [log_left2[d] for d in range(3)]
+        shares, _ = shares_of([unpack_log(g) for g in logs])
+        for k in range(4):
+            share_left2[k] = shares[k]
+        logs = [right_log[x]] + [log_right2[d] for d in range(3)]
+        shares, _ = shares_of([unpack_log(g) for g in logs])
+        for k in range(4):
+            share_right2[k] = shares[k]
 
     def view(i, j, k, cols):
         return all_ref.at[i, j, k, :, cols]
 
-    first = gather_first(copies, own, view, x, y, c, halves)
+    def finish(k, waits):
+        wait_all(waits)
+        for h in range(4):
+            at = k * 512 + h * 128
+            cols = slice(at, at + 128)
+            blocks = [left_now[y, :, cols]] + [in_left2[d, :, cols] for d in range(3)]
+            shares = [share_left2[i] for i in range(4)]
+            own[:, cols] = blended(blocks, shares, k * 4 + h)
+            blocks = [right_now[x, :, cols]] + [in_right2[d, :, cols] for d in range(3)]
+            shares = [share_right2[i] for i in range(4)]
+            own[:, 1024 + at : 1152 + at] = blended(blocks, shares, 8 + k * 4 + h)
+        return gather_first(copies, own, view, x, y, c, chunks[k])
+
+    sums(0, 1, 4, 5)
+    twin0 = to_twin(chunks[0])
+    sums(2, 3)
+    log_wait.wait_recv()
+    lax.fori_loop(0, 4, first_shares, 0)
+    across0, logs = across(0, twin0)
+    sums(6, 7)
+    twin1 = to_twin(chunks[1])
+    across1, _ = across(1, twin1)
+    wait_all(logs)
+    lax.fori_loop(0, 4, second_shares, 0)
+    along0, logs = along(0, across0)
+    along1, _ = along(1, across1)
+    wait_all(logs)
+    third_shares()
+    first = [finish(0, along0), finish(1, along1)]
     all_ref[x, y, c] = own[...]
-    for wait in first:
-        wait.wait_recv()
-    second = gather_second(copies, view, x, y, c, halves)
-    for wait in gather_third(copies, second, view, x, y, c, halves):
-        wait.wait_recv()
+    second, third = [], []
+    for halves, waits in zip(chunks, first):
+        wait_all(waits)
+        second.append(gather_second(copies, view, x, y, c, halves))
+        third += pass_own(copies, view, x, y, c, halves)
+    for halves, waits in zip(chunks, second):
+        third += pass_on(copies, waits, view, x, y, c, halves)
+    wait_all(third)
     attention = all_ref[...].reshape(512, 2048)
     terms[...] = (
         lax.dot_general(
@@ -483,8 +573,7 @@
         for d in (2, 1, 3)
     ]
     out_ref[0] = terms[z]
-    for wait in waits:
-        wait.wait_recv()
+    wait_all(waits)
     copies.drain()
 
 
@@ -521,22 +610,36 @@
             pltpu.VMEM((pages, width), f32),
             pltpu.VMEM((pages, 128), f32),
             pltpu.VMEM((pages, 128), f32),
-            pltpu.VMEM((2, 4, 4, 16, 2304), bf16),
-            pltpu.VMEM((4, 4, 16, 2304), bf16),
-            pltpu.VMEM((4, 4, 16, 2304), bf16),
-            pltpu.VMEM((3, 4, 16, 1152), bf16),
-            pltpu.VMEM((3, 4, 16, 1152), bf16),
-            pltpu.VMEM((4, 16, 1152), bf16),
-            pltpu.VMEM((4, 16, 1152), bf16),
-            pltpu.VMEM((3, 16, 1152), bf16),
-            pltpu.VMEM((3, 16, 1152), bf16),
+            pltpu.VMEM((2, 4, 4, 16, 2048), bf16),
+            pltpu.VMEM((2, 4, 4, 16, 128), bf16),
+            pltpu.VMEM((4, 4, 16, 2048), bf16),
+            pltpu.VMEM((4, 4, 16, 128), bf16),
+            pltpu.VMEM((4, 4, 16, 2048), bf16),
+            pltpu.VMEM((4, 4, 16, 128), bf16),
+            pltpu.VMEM((2, 4, 4, 16, 128), f32),
+            pltpu.VMEM((3, 4, 16, 1024), bf16),
+            pltpu.VMEM((3, 4, 16, 1024), bf16),
+            pltpu.VMEM((3, 4, 16, 128), bf16),
+            pltpu.VMEM((3, 4, 16, 128), bf16),
+            pltpu.VMEM((4, 4, 16, 128), f32),
+            pltpu.VMEM((4, 4, 16, 128), f32),
+            pltpu.VMEM((4, 16, 1024), bf16),
+            pltpu.VMEM((4, 16, 1024), bf16),
+            pltpu.VMEM((4, 16, 128), bf16),
+            pltpu.VMEM((4, 16, 128), bf16),
+            pltpu.VMEM((3, 16, 1024), bf16),
+            pltpu.VMEM((3, 16, 1024), bf16),
+            pltpu.VMEM((3, 16, 128), bf16),
+            pltpu.VMEM((3, 16, 128), bf16),
+            pltpu.VMEM((4, 16, 128), f32),
+            pltpu.VMEM((4, 16, 128), f32),
             pltpu.VMEM((16, 2048), bf16),
             pltpu.VMEM((4, 4, 2, 16, 2048), bf16),
             pltpu.VMEM((4, 64, 512), bf16),
             pltpu.VMEM((256, 2048), bf16),
             pltpu.SemaphoreType.DMA((2,)),
-            pltpu.SemaphoreType.DMA((66,)),
-            pltpu.SemaphoreType.DMA((66,)),
+            pltpu.SemaphoreType.DMA((131,)),
+            pltpu.SemaphoreType.DMA((131,)),
         ],
         compiler_params=pltpu.CompilerParams(
             collective_id=1, has_side_effects=True, vmem_limit_bytes=60 * 1024 * 1024

time: 88.5 us -> 77.8 us (0.88)
  Pallas kernels: 85.2 us -> 74.5 us
    pallas_call x1, Pallas kernels: 85.2 us -> 74.5 us  [whole(): pl.pallas_call(whole_kernel, out_shape=jax.ShapeDtypeStruct((4, 64, 512),...]
where the time goes in v5:
time: 77.8 us; the launch traced here: 77.6 us
  Pallas kernels  74.5 us (96%)
  other arithmetic  1.64 us (2%)
  local copies, waits for them, and re-layouts  1.49 us (2%)
    pallas_call x1, Pallas kernels, whole(): pl.pallas_call(whole_kernel, out_shape=jax.ShapeDtypeStruct((4, 64, 512),...  74.5 us
    reduce_sum x1, other arithmetic, on_device(): return jnp.sum(terms.astype(jnp.float32), axis=0).astype(jnp.bfloat16).T  1.64 us

profile of v5, /device:TPU:1, one launch (start us, length us, event | category | flops | bytes accessed | tf_op | source)
XLA Modules:
  0.0 77.6 jit_solution(15608524464677227874)
XLA Ops:
  0.0 1.5 %copy.11 = bf16[2,8,16,128]{3,1,2,0:T(8,128)(2,1)} copy(bf16[2,8,16,128]{3,2,1,0:T(8,128)(2,1)} %bitcast.12) | data formatting | bytes 131072
  1.5 74.5 %whole.1 = bf16[4,64,512]{2,1,0:T(8,128)(2,1)} custom-call(s32[16]{0:T(128)} %lengths_ref.1, bf16[16,2048]{1,0:T(8,128)(2,1)} %bitcast.11, s32[16,128]{1,0:T(8,128)} %table_ref.1, f32[2,1024]{1,0:T(2,128)} %bitcast.13, f32[2,1024]{1,0:T(2,128)} %bitcast.14, bf16[32768,128]{1,0:T(8,128)(2,1)} %bitcast.9, bf16[32768,128]{1,0:T(8,128)(2,1)} %bitcast.10, ...), custom_call_target="tpu_custom_call" | custom-call | tf_op jit(solution)/shard_map/whole/pallas_call | solution.py:587
  76.0 1.6 %reduce_sum.12 = bf16[64,512]{1,0:T(8,128)(2,1)} reduce(bf16[4,64,512]{2,1,0:T(8,128)(2,1)} %whole.1, bf16[]{:T(256)} %constant.2.clone.1), dimensions={0}, to_apply=%region_0.0 | reduce | flops 98304 | bytes 327682 | tf_op jit(solution)/shard_map/reduce_sum | solution.py:672

commit v6 on v5

--- a/solution.py
+++ b/solution.py
@@ -63,21 +63,23 @@
     lax.fori_loop(0, code_ref.shape[0], body, 0)
 
 
-def page_queries(q_ref, pick_ref, qs_ref):
+def page_queries(k, q_ref, pick_ref, qs_ref):
     f32, bf16 = jnp.float32, jnp.bfloat16
     tiles = qs_ref.shape[0]
 
-    def body(n, carry):
-        cols = pl.ds(pl.multiple_of(n * 256, 256), 256)
-        queries = q_ref[:, :, :, :, cols].reshape(pick_ref.shape[1], 256)
-        got = jnp.dot(pick_ref[...], queries, preferred_element_type=f32)
-        pair = [got[:, j * 128 : (j + 1) * 128].reshape(tiles, 8, 128) for j in range(2)]
-        qs_ref[:, pl.ds(pl.multiple_of(n * 16, 16), 16), :] = jnp.concatenate(
-            pair, axis=1
-        ).astype(bf16)
+    def body(i, carry):
+        for u in range(2):
+            n = i * 4 + 2 * k + u
+            cols = pl.ds(pl.multiple_of(n * 256, 256), 256)
+            queries = q_ref[:, :, :, :, cols].reshape(pick_ref.shape[1], 256)
+            got = jnp.dot(pick_ref[...], queries, preferred_element_type=f32)
+            pair = [got[:, j * 128 : (j + 1) * 128].reshape(tiles, 8, 128) for j in range(2)]
+            qs_ref[:, pl.ds(pl.multiple_of(n * 16, 16), 16), :] = jnp.concatenate(
+                pair, axis=1
+            ).astype(bf16)
         return carry
 
-    lax.fori_loop(0, q_ref.shape[-1] // 256, body, 0)
+    lax.fori_loop(0, 2, body, 0)
 
 
 def page_sums(k_ref, v_ref, wide_ref, qs_ref, s_ref, p_ref, po_ref, pm_ref, ps_ref):
@@ -306,19 +308,19 @@
 
 
 def whole_kernel(
-    lengths_ref, q_ref, table_ref, ks_ref, vs_ref, k_hbm, v_hbm, weight_ref, out_ref,
-    k_ref, v_ref, every_ref, code_ref, table_out, sum_y, sum_c, in_x, in_y, in_c,
+    lengths_ref, queries_ref, table_ref, ks_ref, vs_ref, k_hbm, v_hbm, weight_hbm, out_ref,
+    k_ref, v_ref, weight_ref, wide_q, q_ref, every_ref, code_ref, table_out, sum_y, sum_c, in_x, in_y, in_c,
     rows_ref, wide_ref, pick_ref, pickt_ref, qs_ref, s_ref, p_ref, po_ref, pm_ref, ps_ref,
     part_ref, log_ref, twin_in, log_in, now, now_log, share0,
     in_left, in_right, log_left, log_right, share_left, share_right,
     left_now, right_now, left_log, right_log,
     in_left2, in_right2, log_left2, log_right2, share_left2, share_right2,
-    own, all_ref, terms, turned, load_sems, send_sems, recv_sems,
+    own, all_ref, half_terms, terms, terms_in, turned, load_sems, send_sems, recv_sems,
 ):
     f32, bf16 = jnp.float32, jnp.bfloat16
     x, y, c = place()
     z = lax.axis_index("head")
-    rows, width = q_ref.shape
+    rows = q_ref.shape[0]
     chunks = [
         (slice(k * 512, k * 512 + 512), slice(1024 + k * 512, 1536 + k * 512)) for k in range(2)
     ]
@@ -326,6 +328,8 @@
         pltpu.make_async_copy(k_hbm, k_ref, load_sems.at[0]),
         pltpu.make_async_copy(v_hbm, v_ref, load_sems.at[1]),
     ]
+    load_weight = pltpu.make_async_copy(weight_hbm, weight_ref, load_sems.at[2])
+    load_weight.start()
     for load in loads:
         load.start()
 
@@ -336,6 +340,9 @@
     peers += [chip(x, off(y, d), c) for d in (1, 2, 3)]
     peers += [chip(x, y, 1 - c)] + [{"head": off(z, d)} for d in (1, 2, 3)]
     met = greet(peers)
+    wide_q[...] = queries_ref[...].astype(f32).reshape(wide_q.shape)
+    for h in range(16):
+        q_ref[:, h * 128 : (h + 1) * 128] = wide_q[pl.ds(h, rows, stride=16), :].astype(bf16)
     copies = Copies(send_sems, recv_sems)
     lane = lax.broadcasted_iota(jnp.int32, (1, 128), 1)
     high_id = lax.broadcasted_iota(jnp.int32, (256, 128), 0)
@@ -372,18 +379,21 @@
     for halves, waits in zip(chunks, first):
         wait_all(waits)
         second.append(gather_second(copies, view_all, x, y, c, halves))
-        third += pass_own(copies, view_all, x, y, c, halves)
+        third.append(pass_own(copies, view_all, x, y, c, halves))
     wait_all(got)
     sum_c[...] = sum_y[y] + in_y[0] + in_y[1] + in_y[2]
     copies.send(sum_c.at[1 - c], in_c, chip(x, y, 1 - c), in_c).wait_recv()
     code_ref[...] = sum_c[c] + in_c[...] - 1.0
     page_columns(code_ref, ks_ref, vs_ref, rows_ref, wide_ref, pick_ref, pickt_ref)
+    load_weight.wait()
     for k in range(16):
         turned[:, k * 128 : (k + 1) * 128] = weight_ref[k * 128 : (k + 1) * 128, :].T
-    for halves, waits in zip(chunks, second):
-        third += pass_on(copies, waits, view_all, x, y, c, halves)
-    wait_all(third)
-    page_queries(every_ref, pick_ref, qs_ref)
+    third[0] += pass_on(copies, second[0], view_all, x, y, c, chunks[0])
+    wait_all(third[0])
+    page_queries(0, every_ref, pick_ref, qs_ref)
+    third[1] += pass_on(copies, second[1], view_all, x, y, c, chunks[1])
+    wait_all(third[1])
+    page_queries(1, every_ref, pick_ref, qs_ref)
     for load in loads:
         load.wait()
     page_sums(k_ref, v_ref, wide_ref, qs_ref, s_ref, p_ref, po_ref, pm_ref, ps_ref)
@@ -556,42 +566,61 @@
     for halves, waits in zip(chunks, first):
         wait_all(waits)
         second.append(gather_second(copies, view, x, y, c, halves))
-        third += pass_own(copies, view, x, y, c, halves)
-    for halves, waits in zip(chunks, second):
-        third += pass_on(copies, waits, view, x, y, c, halves)
-    wait_all(third)
-    attention = all_ref[...].reshape(512, 2048)
-    terms[...] = (
-        lax.dot_general(
-            turned[...], attention, (((1,), (1,)), ((), ())), preferred_element_type=f32
+        third.append(pass_own(copies, view, x, y, c, halves))
+
+    def product(k, i):
+        total = jnp.zeros((256, 256), f32)
+        for cols in chunks[k]:
+            total = total + lax.dot_general(
+                turned[:, cols], all_ref[2 * i : 2 * i + 2, :, :, :, cols].reshape(256, 512),
+                (((1,), (1,)), ((), ())), preferred_element_type=f32,
+            )
+        return total
+
+    third[0] += pass_on(copies, second[0], view, x, y, c, chunks[0])
+    wait_all(third[0])
+    for i in range(2):
+        half_terms[:, i * 256 : i * 256 + 256] = product(0, i)
+    third[1] += pass_on(copies, second[1], view, x, y, c, chunks[1])
+    wait_all(third[1])
+    waits = []
+    for i in range(2):
+        cols = slice(i * 256, i * 256 + 256)
+        terms[:, :, cols] = (
+            (half_terms[:, cols] + product(1, i)).astype(bf16).reshape(4, 64, 256)
         )
-        .astype(bf16)
-        .reshape(4, 64, 512)
-    )
-    waits = [
-        copies.send(terms.at[off(z, d)], out_ref.at[d], {"head": off(z, d)}, out_ref.at[d])
-        for d in (2, 1, 3)
-    ]
-    out_ref[0] = terms[z]
+        for d in (2, 1, 3):
+            here = terms_in.at[d - 1, :, cols]
+            waits.append(
+                copies.send(terms.at[off(z, d), :, cols], here, {"head": off(z, d)}, here)
+            )
     wait_all(waits)
+    total = terms[z].astype(f32)
+    for d in range(3):
+        total = total + terms_in[d].astype(f32)
+    out_ref[...] = total.astype(bf16)
     copies.drain()
 
 
 def whole(lengths, queries, page_table, ks, vs, keys, values, weight):
     f32, bf16 = jnp.float32, jnp.bfloat16
-    rows, width = queries.shape
+    rows = queries.shape[0]
+    width = queries.shape[1] * queries.shape[2]
     pages = keys.shape[0] // 32
     requests = 32 * rows
     vmem = pl.BlockSpec(memory_space=pltpu.VMEM)
     hbm = pl.BlockSpec(memory_space=pl.ANY)
     return pl.pallas_call(
         whole_kernel,
-        out_shape=jax.ShapeDtypeStruct((4, 64, 512), bf16),
-        in_specs=[pl.BlockSpec(memory_space=pltpu.SMEM), vmem, vmem, vmem, vmem, hbm, hbm, vmem],
+        out_shape=jax.ShapeDtypeStruct((64, 512), bf16),
+        in_specs=[pl.BlockSpec(memory_space=pltpu.SMEM), vmem, vmem, vmem, vmem, hbm, hbm, hbm],
         out_specs=vmem,
         scratch_shapes=[
             pltpu.VMEM(keys.shape, bf16),
             pltpu.VMEM(keys.shape, bf16),
+            pltpu.VMEM(weight.shape, bf16),
+            pltpu.VMEM((rows * 16, 128), f32),
+            pltpu.VMEM((rows, width), bf16),
             pltpu.VMEM((2, 4, 4, rows, width), bf16),
             pltpu.VMEM((8, 128), f32),
             pltpu.VMEM((4, 4, 2, 8, 128), f32),
@@ -635,11 +664,13 @@
             pltpu.VMEM((4, 16, 128), f32),
             pltpu.VMEM((16, 2048), bf16),
             pltpu.VMEM((4, 4, 2, 16, 2048), bf16),
+            pltpu.VMEM((256, 512), f32),
             pltpu.VMEM((4, 64, 512), bf16),
+            pltpu.VMEM((3, 64, 512), bf16),
             pltpu.VMEM((256, 2048), bf16),
-            pltpu.SemaphoreType.DMA((2,)),
-            pltpu.SemaphoreType.DMA((131,)),
-            pltpu.SemaphoreType.DMA((131,)),
+            pltpu.SemaphoreType.DMA((3,)),
+            pltpu.SemaphoreType.DMA((134,)),
+            pltpu.SemaphoreType.DMA((134,)),
         ],
         compiler_params=pltpu.CompilerParams(
             collective_id=1, has_side_effects=True, vmem_limit_bytes=60 * 1024 * 1024
@@ -659,17 +690,16 @@
     out_weight,
 ):
     head_size = k_codes.shape[-1]
-    terms = whole(
+    return whole(
         lengths,
-        queries.reshape(queries.shape[0], -1),
+        queries,
         page_table,
         key_page_scale.T,
         value_page_scale.T,
         k_codes.reshape(-1, head_size),
         value_quantized_codes.reshape(-1, head_size),
         out_weight,
-    )
-    return jnp.sum(terms.astype(jnp.float32), axis=0).astype(jnp.bfloat16).T
+    ).T
 
 
 def solution(mesh):

time: 77.8 us -> 76.4 us (0.982)
  other arithmetic: 1.64 us -> 0 us
    reduce_sum x1 -> x0, other arithmetic: 1.64 us -> none  [on_device(): return jnp.sum(terms.astype(jnp.float32), axis=0).astype(jnp.bfloat16).T]
where the time goes in v6:
time: 76.4 us; the launch traced here: 76.2 us
  Pallas kernels  74.7 us (98%)
  local copies, waits for them, and re-layouts  1.47 us (2%)
    pallas_call x1, Pallas kernels, whole(): pl.pallas_call(whole_kernel, out_shape=jax.ShapeDtypeStruct((64, 512), bf...  74.7 us

profile of v6, /device:TPU:1, one launch (start us, length us, event | category | flops | bytes accessed | tf_op | source)
XLA Modules:
  0.0 76.2 jit_solution(6252612941947097999)
XLA Ops:
  0.0 74.7 %whole.1 = bf16[64,512]{1,0:T(8,128)(2,1)} custom-call(s32[16]{0:T(128)} %lengths_ref.1, bf16[16,16,128]{2,1,0:T(8,128)(2,1)} %queries_ref.1, s32[16,128]{1,0:T(8,128)} %table_ref.1, f32[2,1024]{1,0:T(2,128)} %bitcast.8, f32[2,1024]{1,0:T(2,128)} %bitcast.9, bf16[32768,128]{1,0:T(8,128)(2,1)} %bitcast.5, bf16[32768,128]{1,0:T(8,128)(2,1)} %bitcast.6, ...), custom_call_target="tpu_custom_call" | custom-call | tf_op jit(solution)/shard_map/whole/pallas_call | solution.py:613
  74.7 1.5 %copy.10 = bf16[512,64]{0,1:T(8,128)(2,1)} copy(bf16[512,64]{0,1:T(8,128)(2,1)} %bitcast.7) | data formatting | bytes 131072

commit v7 on v6

--- a/solution.py
+++ b/solution.py
@@ -174,7 +174,7 @@
     f32, bf16 = jnp.float32, jnp.bfloat16
     cols = [
         (po_ref[:, h * 128 : (h + 1) * 128] * ps_ref[:, h : h + 1]).astype(bf16)
-        for h in (2 * n, 2 * n + 1)
+        for h in range(4 * n, 4 * n + 4)
     ]
     return jnp.dot(
         pickt_ref[...], jnp.concatenate(cols, axis=1), preferred_element_type=f32
@@ -385,13 +385,10 @@
     copies.send(sum_c.at[1 - c], in_c, chip(x, y, 1 - c), in_c).wait_recv()
     code_ref[...] = sum_c[c] + in_c[...] - 1.0
     page_columns(code_ref, ks_ref, vs_ref, rows_ref, wide_ref, pick_ref, pickt_ref)
-    load_weight.wait()
-    for k in range(16):
-        turned[:, k * 128 : (k + 1) * 128] = weight_ref[k * 128 : (k + 1) * 128, :].T
     third[0] += pass_on(copies, second[0], view_all, x, y, c, chunks[0])
+    third[1] += pass_on(copies, second[1], view_all, x, y, c, chunks[1])
     wait_all(third[0])
     page_queries(0, every_ref, pick_ref, qs_ref)
-    third[1] += pass_on(copies, second[1], view_all, x, y, c, chunks[1])
     wait_all(third[1])
     page_queries(1, every_ref, pick_ref, qs_ref)
     for load in loads:
@@ -405,9 +402,9 @@
 
     def sums(*pairs):
         for n in pairs:
-            part_ref[:, :, :, :, n * 256 : n * 256 + 256] = request_sums(
+            part_ref[:, :, :, :, n * 512 : n * 512 + 512] = request_sums(
                 n, pickt_ref, po_ref, ps_ref
-            ).reshape(2, 4, 4, rows, 256)
+            ).reshape(2, 4, 4, rows, 512)
 
     def to_twin(halves):
         return [
@@ -545,15 +542,18 @@
             own[:, 1024 + at : 1152 + at] = blended(blocks, shares, 8 + k * 4 + h)
         return gather_first(copies, own, view, x, y, c, chunks[k])
 
-    sums(0, 1, 4, 5)
+    sums(0, 2)
     twin0 = to_twin(chunks[0])
-    sums(2, 3)
+    sums(1)
     log_wait.wait_recv()
     lax.fori_loop(0, 4, first_shares, 0)
     across0, logs = across(0, twin0)
-    sums(6, 7)
+    sums(3)
     twin1 = to_twin(chunks[1])
     across1, _ = across(1, twin1)
+    load_weight.wait()
+    for k in range(16):
+        turned[:, k * 128 : (k + 1) * 128] = weight_ref[k * 128 : (k + 1) * 128, :].T
     wait_all(logs)
     lax.fori_loop(0, 4, second_shares, 0)
     along0, logs = along(0, across0)
@@ -578,10 +578,10 @@
         return total
 
     third[0] += pass_on(copies, second[0], view, x, y, c, chunks[0])
+    third[1] += pass_on(copies, second[1], view, x, y, c, chunks[1])
     wait_all(third[0])
     for i in range(2):
         half_terms[:, i * 256 : i * 256 + 256] = product(0, i)
-    third[1] += pass_on(copies, second[1], view, x, y, c, chunks[1])
     wait_all(third[1])
     waits = []
     for i in range(2):

time: 76.4 us -> 74.5 us (0.975)
  Pallas kernels: 74.7 us -> 72.9 us
    pallas_call x1, Pallas kernels: 74.7 us -> 72.9 us  [whole(): pl.pallas_call(whole_kernel, out_shape=jax.ShapeDtypeStruct((64, 512), bf...]
where the time goes in v7:
time: 74.5 us; the launch traced here: 74.4 us
  Pallas kernels  72.9 us (98%)
  local copies, waits for them, and re-layouts  1.47 us (2%)
    pallas_call x1, Pallas kernels, whole(): pl.pallas_call(whole_kernel, out_shape=jax.ShapeDtypeStruct((64, 512), bf...  72.9 us

profile of v7, /device:TPU:1, one launch (start us, length us, event | category | flops | bytes accessed | tf_op | source)
XLA Modules:
  0.0 74.4 jit_solution(9767926545051963298)
XLA Ops:
  0.0 72.9 %whole.1 = bf16[64,512]{1,0:T(8,128)(2,1)} custom-call(s32[16]{0:T(128)} %lengths_ref.1, bf16[16,16,128]{2,1,0:T(8,128)(2,1)} %queries_ref.1, s32[16,128]{1,0:T(8,128)} %table_ref.1, f32[2,1024]{1,0:T(2,128)} %bitcast.8, f32[2,1024]{1,0:T(2,128)} %bitcast.9, bf16[32768,128]{1,0:T(8,128)(2,1)} %bitcast.5, bf16[32768,128]{1,0:T(8,128)(2,1)} %bitcast.6, ...), custom_call_target="tpu_custom_call" | custom-call | tf_op jit(solution)/shard_map/whole/pallas_call | solution.py:613
  72.9 1.5 %copy.10 = bf16[512,64]{0,1:T(8,128)(2,1)} copy(bf16[512,64]{0,1:T(8,128)(2,1)} %bitcast.7) | data formatting | bytes 131072

commit v8 on v7

--- a/solution.py
+++ b/solution.py
@@ -138,12 +138,14 @@
 
     def body(i, carry):
         for u in range(UNROLL):
-            values(u, jnp.maximum(i - 2, 0) * UNROLL + u)
-            soften(u, jnp.clip(i - 1, 0, groups - 1) * UNROLL + u)
             scores(u, jnp.minimum(i, groups - 1) * UNROLL + u)
+        for u in range(UNROLL):
+            values(u, jnp.maximum(i - 1, 0) * UNROLL + u)
+        for u in range(UNROLL):
+            soften(u, jnp.minimum(i, groups - 1) * UNROLL + u)
         return carry
 
-    lax.fori_loop(0, groups + 2, body, 0)
+    lax.fori_loop(0, groups + 1, body, 0)
 
 
 def unpack_log(aux):

time: 74.5 us -> 73.7 us (0.989)
  Pallas kernels: 72.9 us -> 72 us
    pallas_call x1, Pallas kernels: 72.9 us -> 72 us  [whole(): pl.pallas_call(whole_kernel, out_shape=jax.ShapeDtypeStruct((64, 512), bf...]
where the time goes in v8:
time: 73.7 us; the launch traced here: 73.5 us
  Pallas kernels  72 us (98%)
  local copies, waits for them, and re-layouts  1.47 us (2%)
    pallas_call x1, Pallas kernels, whole(): pl.pallas_call(whole_kernel, out_shape=jax.ShapeDtypeStruct((64, 512), bf...  72 us

profile of v8, /device:TPU:1, one launch (start us, length us, event | category | flops | bytes accessed | tf_op | source)
XLA Modules:
  0.0 73.5 jit_solution(8671854501211828025)
XLA Ops:
  0.0 72.0 %whole.1 = bf16[64,512]{1,0:T(8,128)(2,1)} custom-call(s32[16]{0:T(128)} %lengths_ref.1, bf16[16,16,128]{2,1,0:T(8,128)(2,1)} %queries_ref.1, s32[16,128]{1,0:T(8,128)} %table_ref.1, f32[2,1024]{1,0:T(2,128)} %bitcast.8, f32[2,1024]{1,0:T(2,128)} %bitcast.9, bf16[32768,128]{1,0:T(8,128)(2,1)} %bitcast.5, bf16[32768,128]{1,0:T(8,128)(2,1)} %bitcast.6, ...), custom_call_target="tpu_custom_call" | custom-call | tf_op jit(solution)/shard_map/whole/pallas_call | solution.py:615
  72.0 1.5 %copy.10 = bf16[512,64]{0,1:T(8,128)(2,1)} copy(bf16[512,64]{0,1:T(8,128)(2,1)} %bitcast.7) | data formatting | bytes 131072

commit v9 on v8

--- a/solution.py
+++ b/solution.py
@@ -67,19 +67,11 @@
     f32, bf16 = jnp.float32, jnp.bfloat16
     tiles = qs_ref.shape[0]
 
-    def body(i, carry):
-        for u in range(2):
-            n = i * 4 + 2 * k + u
-            cols = pl.ds(pl.multiple_of(n * 256, 256), 256)
-            queries = q_ref[:, :, :, :, cols].reshape(pick_ref.shape[1], 256)
-            got = jnp.dot(pick_ref[...], queries, preferred_element_type=f32)
-            pair = [got[:, j * 128 : (j + 1) * 128].reshape(tiles, 8, 128) for j in range(2)]
-            qs_ref[:, pl.ds(pl.multiple_of(n * 16, 16), 16), :] = jnp.concatenate(
-                pair, axis=1
-            ).astype(bf16)
-        return carry
-
-    lax.fori_loop(0, 2, body, 0)
+    for n in (2 * k, 2 * k + 1, 2 * k + 4, 2 * k + 5):
+        queries = q_ref[:, :, :, :, n * 256 : n * 256 + 256].reshape(pick_ref.shape[1], 256)
+        got = jnp.dot(pick_ref[...], queries, preferred_element_type=f32)
+        pair = [got[:, j * 128 : (j + 1) * 128].reshape(tiles, 8, 128) for j in range(2)]
+        qs_ref[:, n * 16 : n * 16 + 16, :] = jnp.concatenate(pair, axis=1).astype(bf16)
 
 
 def page_sums(k_ref, v_ref, wide_ref, qs_ref, s_ref, p_ref, po_ref, pm_ref, ps_ref):
@@ -174,8 +166,13 @@
 
 def request_sums(n, pickt_ref, po_ref, ps_ref):
     f32, bf16 = jnp.float32, jnp.bfloat16
+    share = ps_ref[...].astype(bf16)
+    wide = (po_ref.shape[0], 128)
     cols = [
-        (po_ref[:, h * 128 : (h + 1) * 128] * ps_ref[:, h : h + 1]).astype(bf16)
+        (
+            po_ref[:, h * 128 : (h + 1) * 128]
+            * jnp.broadcast_to(share[:, h : h + 1], wide).astype(f32)
+        ).astype(bf16)
         for h in range(4 * n, 4 * n + 4)
     ]
     return jnp.dot(

time: 73.7 us -> 72.2 us (0.980)
  Pallas kernels: 72 us -> 70.5 us
    pallas_call x1, Pallas kernels: 72 us -> 70.5 us  [whole(): pl.pallas_call(whole_kernel, out_shape=jax.ShapeDtypeStruct((64, 512), bf...]
where the time goes in v9:
time: 72.2 us; the launch traced here: 72 us
  Pallas kernels  70.5 us (98%)
  local copies, waits for them, and re-layouts  1.47 us (2%)
    pallas_call x1, Pallas kernels, whole(): pl.pallas_call(whole_kernel, out_shape=jax.ShapeDtypeStruct((64, 512), bf...  70.5 us
    unnamed x1, local copies, waits for them, and re-layouts  1.47 us

profile of v9, /device:TPU:1, one launch (start us, length us, event | category | flops | bytes accessed | tf_op | source)
XLA Modules:
  0.0 72.0 jit_solution(2548871112316244436)
XLA Ops:
  0.0 70.5 %whole.1 = bf16[64,512]{1,0:T(8,128)(2,1)} custom-call(s32[16]{0:T(128)} %lengths_ref.1, bf16[16,16,128]{2,1,0:T(8,128)(2,1)} %queries_ref.1, s32[16,128]{1,0:T(8,128)} %table_ref.1, f32[2,1024]{1,0:T(2,128)} %bitcast.8, f32[2,1024]{1,0:T(2,128)} %bitcast.9, bf16[32768,128]{1,0:T(8,128)(2,1)} %bitcast.5, bf16[32768,128]{1,0:T(8,128)(2,1)} %bitcast.6, ...), custom_call_target="tpu_custom_call" | custom-call | tf_op jit(solution)/shard_map/whole/pallas_call | solution.py:612
  70.5 1.5 %copy.10 = bf16[512,64]{0,1:T(8,128)(2,1)} copy(bf16[512,64]{0,1:T(8,128)(2,1)} %bitcast.7) | data formatting | bytes 131072
